TPU v7x, 16 devices: a whole 2x2x2 slice. The times are simulated.
16 devices in a mesh: ep: 16 (over z, y, x, core).
Axes of the slice: x: 2, y: 2, z: 2, core: 2. Of those that a mesh axis runs over, the one named last changes fastest.
Arguments:
- x_tok: bfloat16 [24576, 1024], P('ep')
- route_idx: int32 [24576, 8], P('ep')
- gates: bfloat16 [24576, 8], P('ep')
- dy_tok: bfloat16 [24576, 1024], P('ep')
- w_gate: bfloat16 [32, 1024, 512], P('ep')
- w_up: bfloat16 [32, 1024, 512], P('ep')
- w_down: bfloat16 [32, 512, 1024], P('ep')
Outputs:
- output 1: bfloat16 [24576, 1024], P('ep')
- output 2: bfloat16 [24576, 1024], P('ep')
- output 3: float32 [32, 1024, 512], P('ep')
- output 4: float32 [32, 1024, 512], P('ep')
- output 5: float32 [32, 512, 1024], P('ep')
All inputs are finite; a program needn't handle non-finite values.
Results may differ from a plain program's by a relative error of at most 0.0104009.
Values are sent between devices in bfloat16 or wider.
A program may use at most 1 GiB of HBM per device.

v0:
```python
import jax
import jax.numpy as jnp
from jax import lax
from jax.sharding import PartitionSpec as P

HOLDERS = 4


def holder_table(n_dev):
    quarter = n_dev // 4
    return jnp.array([[0, quarter, n_dev // 2, 3 * quarter], [n_dev - 1, n_dev // 2, 3 * quarter, quarter - 1]], jnp.int32)


def plan_slots(route_loc, gate_loc, n_dev, per_dev, slot_cap, hot_rows):
    tok_loc, top_k = route_loc.shape
    experts = per_dev * n_dev
    reg_rows = per_dev * slot_cap
    block_rows = reg_rows + 2 * hot_rows
    flat_route = route_loc.reshape(-1)
    onehot = (flat_route[:, None] == jnp.arange(experts, dtype=jnp.int32)[None, :]).astype(jnp.int32)
    expert_rank = jnp.sum((jnp.cumsum(onehot, axis=0) - 1) * onehot, axis=1)
    second_hot = (flat_route == experts - 1).astype(jnp.int32)
    is_hot = (flat_route == 0) | (flat_route == experts - 1)
    dest_hot = holder_table(n_dev)[second_hot, expert_rank % HOLDERS]
    offset_hot = reg_rows + second_hot * hot_rows + expert_rank // HOLDERS
    dest_dev = jnp.where(is_hot, dest_hot, flat_route // per_dev)
    offset = jnp.where(is_hot, offset_hot, (flat_route % per_dev) * slot_cap + expert_rank)
    slot_idx = dest_dev * block_rows + offset
    total_slots = n_dev * block_rows
    token_ids = jnp.arange(tok_loc * top_k, dtype=jnp.int32) // top_k
    src_tok = jnp.full((total_slots,), tok_loc, jnp.int32).at[slot_idx].set(token_ids)
    src_gate = jnp.zeros((total_slots,), gate_loc.dtype).at[slot_idx].set(gate_loc.reshape(-1))
    return slot_idx.reshape(tok_loc, top_k), src_tok, src_gate


def expert_forward(in_rows, gate_w, up_w, down_w):
    u_val = jnp.einsum('secd,edf->secf', in_rows, gate_w, preferred_element_type=jnp.float32)
    v_val = jnp.einsum('secd,edf->secf', in_rows, up_w, preferred_element_type=jnp.float32)
    sig_u = jax.nn.sigmoid(u_val)
    act_rows = (u_val * sig_u * v_val).astype(jnp.bfloat16)
    out_rows = jnp.einsum('secf,efd->secd', act_rows, down_w, preferred_element_type=jnp.float32).astype(jnp.bfloat16)
    return out_rows, (u_val, v_val, sig_u, act_rows)


def expert_backward(in_rows, d_out, saved_acts, gate_w, up_w, down_w):
    u_val, v_val, sig_u, act_rows = saved_acts
    d_act = jnp.einsum('secd,efd->secf', d_out, down_w, preferred_element_type=jnp.float32)
    d_u = (d_act * v_val * sig_u * (1.0 + u_val * (1.0 - sig_u))).astype(jnp.bfloat16)
    d_v = (d_act * u_val * sig_u).astype(jnp.bfloat16)
    d_rows = (jnp.einsum('secf,edf->secd', d_u, gate_w, preferred_element_type=jnp.float32) + jnp.einsum('secf,edf->secd', d_v, up_w, preferred_element_type=jnp.float32)).astype(jnp.bfloat16)
    g_gate = jnp.einsum('secd,secf->edf', in_rows, d_u, preferred_element_type=jnp.float32)
    g_up = jnp.einsum('secd,secf->edf', in_rows, d_v, preferred_element_type=jnp.float32)
    g_down = jnp.einsum('secf,secd->efd', act_rows, d_out, preferred_element_type=jnp.float32)
    return d_rows, g_gate, g_up, g_down


def solution(mesh):
    n_dev = mesh.shape['ep']

    def local_step(x_tok, route_idx, gates, dy_tok, w_gate, w_up, w_down):
        tok_loc, top_k = route_idx.shape
        per_dev, model_dim = w_gate.shape[0], w_gate.shape[1]
        experts = per_dev * n_dev
        slot_cap = 2 * tok_loc * top_k // (experts - 2)
        hot_rows = tok_loc // 2 // HOLDERS
        reg_rows = per_dev * slot_cap
        block_rows = reg_rows + 2 * hot_rows
        slot_idx, src_tok, src_gate = plan_slots(route_idx, gates, n_dev, per_dev, slot_cap, hot_rows)
        my_index = lax.axis_index('ep')
        owner_one = my_index == 0
        owner_two = my_index == n_dev - 1

        def hot_copy(weights):
            first_copy = jnp.where(owner_one, weights[0], jnp.zeros_like(weights[0]))
            second_copy = jnp.where(owner_two, weights[per_dev - 1], jnp.zeros_like(weights[0]))
            return lax.psum(jnp.stack([first_copy, second_copy]), 'ep')

        hot_gate = hot_copy(w_gate)
        hot_up = hot_copy(w_up)
        hot_down = hot_copy(w_down)

        def exchange(send_rows):
            return lax.all_to_all(send_rows.reshape(n_dev, block_rows, model_dim), 'ep', 0, 0)

        def split_recv(recv_rows):
            reg_part = recv_rows[:, :reg_rows].reshape(n_dev, per_dev, slot_cap, model_dim)
            hot_part = recv_rows[:, reg_rows:].reshape(n_dev, 2, hot_rows, model_dim)
            return reg_part, hot_part

        def join_send(reg_part, hot_part):
            return jnp.concatenate([reg_part.reshape(n_dev, reg_rows, model_dim), hot_part.reshape(n_dev, 2 * hot_rows, model_dim)], axis=1)

        x_reg, x_hot = split_recv(exchange(jnp.take(x_tok, src_tok, axis=0, mode='fill', fill_value=0)))
        o_reg, saved_reg = expert_forward(x_reg, w_gate, w_up, w_down)
        o_hot, saved_hot = expert_forward(x_hot, hot_gate, hot_up, hot_down)
        o_back = exchange(join_send(o_reg, o_hot)).reshape(n_dev * block_rows, model_dim)
        y_tok = jnp.einsum('tk,tkd->td', gates, jnp.take(o_back, slot_idx, axis=0), preferred_element_type=jnp.float32).astype(jnp.bfloat16)

        dy_send = jnp.take(dy_tok, src_tok, axis=0, mode='fill', fill_value=0) * src_gate[:, None]
        d_reg, d_hot = split_recv(exchange(dy_send))
        dx_reg, g_gate, g_up, g_down = expert_backward(x_reg, d_reg, saved_reg, w_gate, w_up, w_down)
        dx_hot, h_gate, h_up, h_down = expert_backward(x_hot, d_hot, saved_hot, hot_gate, hot_up, hot_down)
        dx_back = exchange(join_send(dx_reg, dx_hot)).reshape(n_dev * block_rows, model_dim)
        dx_tok = jnp.sum(jnp.take(dx_back, slot_idx, axis=0), axis=1, dtype=jnp.float32).astype(jnp.bfloat16)

        h_gate, h_up, h_down = lax.psum((h_gate, h_up, h_down), 'ep')
        local_ids = jnp.arange(per_dev)
        mask_one = ((local_ids == 0) & owner_one).astype(jnp.float32)[:, None, None]
        mask_two = ((local_ids == per_dev - 1) & owner_two).astype(jnp.float32)[:, None, None]

        def settle(local_grad, hot_grad):
            return local_grad + mask_one * hot_grad[0] + mask_two * hot_grad[1]

        return y_tok, dx_tok, settle(g_gate, h_gate), settle(g_up, h_up), settle(g_down, h_down)

    return jax.shard_map(local_step, mesh=mesh, in_specs=(P('ep'), P('ep'), P('ep'), P('ep'), P('ep'), P('ep'), P('ep')), out_specs=(P('ep'), P('ep'), P('ep'), P('ep'), P('ep')), check_vma=False)
```

profile of v0, /device:TPU:0, one launch (start us, length us, event | category | flops | bytes accessed | tf_op | source)
XLA Modules:
  0.0 5630.5 jit_solution(11900984889827597391)
XLA Ops:
  40.6 102.6 %gather_fusion = s32[12288]{0:T(1024)S(1)} fusion(s32[2,4]{1,0:T(2,128)S(1)} %copy-done.2, s32[12288]{0:T(1024)S(1)} %bitcast.220), kind=kCustom, calls=%fused_computation.4 | custom fusion | bytes 196608 | tf_op jit(solution)/shard_map/gather | solution.py:24
  190.4 97.7 %gather_fusion.1 = bf16[32352,1024]{1,0:T(8,128)(2,1)} fusion(bf16[1536,1024]{1,0:T(8,128)(2,1)S(1)} %copy-done, s32[32768]{0:T(1024)S(1)} %pad_clamp_fusion), kind=kCustom, calls=%fused_computation.clone | custom fusion | bytes 132643200 | tf_op jit(solution)/shard_map/jit(_take)/gather | solution.py:93
  288.1 140.4 %gather_fusion.3 = bf16[32352,1024]{1,0:T(8,128)(2,1)} fusion(bf16[1536,1024]{1,0:T(8,128)(2,1)} %param.15, s32[32768]{0:T(1024)S(1)} %pad_clamp_fusion), kind=kCustom, calls=%fused_computation.2.clone | custom fusion | bytes 132643200 | tf_op jit(solution)/shard_map/jit(_take)/gather | solution.py:99
  429.1 85.1 %scatter_custom_fusion.1 = bf16[32352]{0:T(1024)(128)(2,1)S(1)} fusion(s32[12288]{0:T(1024)} %bitcast.245, bf16[12288]{0:T(1024)(128)(2,1)S(1)} %reshape.415, bf16[]{:T(256)} %constant.121.clone.1), kind=kCustom, calls=%fused_computation.186 | custom fusion | bytes 65216 | tf_op jit(solution)/shard_map/scatter | solution.py:32
  514.2 86.1 %select_multiply_fusion = (bf16[32352,1024]{1,0:T(8,128)(2,1)}, bf16[32352,1024]{1,0:T(8,128)(2,1)}) fusion(bf16[32352,1024]{1,0:T(8,128)(2,1)} %gather_fusion.3, pred[32352]{0:T(1024)(128)(4,1)S(1)} %copy-done.14, bf16[32352]{0:T(1024)(128)(2,1)S(1)} %scatter_custom_fusion.1, bf16[32352,1024]{1,0:T(8,128)(2,1)} %gather_fusion.1), kind=kLoop, calls=%fused_computation.10 | loop fusion | flops 99385344 | bytes 265124640 | tf_op jit(solution)/shard_map/mul | solution.py:99
  600.3 62.7 %reshape.352 = bf16[16,2022,1024]{2,1,0:T(8,128)(2,1)} reshape(bf16[32352,1024]{1,0:T(8,128)(2,1)} %get-tuple-element.34) | data formatting | bytes 132513792 | tf_op jit(solution)/shard_map/reshape | solution.py:83
  669.0 62.9 %reshape.359 = bf16[16,2022,1024]{2,1,0:T(8,128)(2,1)} reshape(bf16[32352,1024]{1,0:T(8,128)(2,1)} %get-tuple-element.33) | data formatting | bytes 132513792 | tf_op jit(solution)/shard_map/reshape | solution.py:83
  731.9 718.6 %all-to-all-done = bf16[16,2022,1024]{2,1,0:T(8,128)(2,1)} async-done(((bf16[16,2022,1024]{2,1,0:T(8,128)(2,1)}), bf16[16,2022,1024]{2,1,0:T(8,128)(2,1)}, u32[]{:S(2)}, u32[]{:S(2)}) %all-to-all-start) | async-done | bytes 66256928 | tf_op jit(solution)/shard_map/all_to_all | solution.py:83
  1501.7 113.3 %copy.103 = bf16[16,1638,1024]{2,0,1:T(8,128)(2,1)} copy(bf16[16,1638,1024]{2,1,0:T(8,128)(2,1)} %slice.84) | data formatting | bytes 107347968 | tf_op jit(solution)/shard_map/slice | solution.py:86
  1626.8 647.1 %all-reduce.7.cloned.1.call-done = (bf16[2,1024,512]{2,1,0:T(8,128)(2,1)}, bf16[2,1024,512]{2,1,0:T(8,128)(2,1)}, bf16[2,512,1024]{2,1,0:T(8,128)(2,1)}) async-done(((bf16[2,1024,512]{2,1,0:T(8,128)(2,1)}, bf16[2,1024,512]{2,1,0:T(8,128)(2,1)}, bf16[2,512,1024]{2,1,0:T(8,128)(2,1)}), (bf16[2,1024,512]{2,1,0:T(8,128)(2,1)}, bf16[2,1024,512]{2,1,0:T(8,128)(2,1)}, ...) | async-done | bytes 6291472 | tf_op jit(solution)/shard_map/psum | solution.py:76
  2302.8 91.2 %fusion.15 = f32[2,16,819,512]{3,2,1,0:T(8,128)} fusion(bf16[16,2,819,1024]{3,0,2,1:T(8,128)(2,1)} %bitcast.223, bf16[2,1024,512]{2,1,0:T(8,128)(2,1)} %param.17), kind=kOutput, calls=%fused_computation.34 | convolution fusion | flops 27481079808 | bytes 109445120 | tf_op jit(solution)/shard_map/secd,edf->secf/dot_general | solution.py:38
  2394.0 90.9 %fusion.17 = f32[2,16,819,512]{3,2,1,0:T(8,128)} fusion(bf16[16,2,819,1024]{3,0,2,1:T(8,128)(2,1)} %bitcast.224, bf16[2,1024,512]{2,1,0:T(8,128)(2,1)S(1)} %copy-done.5), kind=kOutput, calls=%fused_computation.36 | convolution fusion | flops 27481079808 | bytes 109445120 | tf_op jit(solution)/shard_map/secd,edf->secf/dot_general | solution.py:37
  2520.3 113.3 %copy.115 = bf16[16,1638,1024]{2,0,1:T(8,128)(2,1)} copy(bf16[16,1638,1024]{2,1,0:T(8,128)(2,1)} %slice.86) | data formatting | bytes 107347968 | tf_op jit(solution)/shard_map/slice | solution.py:86
  2633.6 112.4 %fusion.5 = (bf16[16,2,819,512]{3,2,0,1:T(8,128)(2,1)}, bf16[16,2,819,512]{3,2,0,1:T(8,128)(2,1)}, bf16[16,2,819,512]{3,2,0,1:T(8,128)(2,1)}) fusion(f32[2,16,819,512]{3,2,1,0:T(8,128)} %fusion.17, f32[2,16,819,512]{3,2,1,0:T(8,128)} %fusion.15, bf16[2,512,1024]{2,1,0:T(8,128)(2,1)} %param.18, bf16[16,2,819,1024]{3,0,2,1:T(8,128)(2,1)} %bitcast.227), kind=kOutput, calls=%fused_computation.19 | convolution fusion | flops 27695775744 | bytes 243630080 | tf_op jit(solution)/shard_map/secd,efd->secf/dot_general | solution.py:47
  2794.7 62.6 %fusion = bf16[16,2,819,1024]{3,2,0,1:T(8,128)(2,1)} fusion(f32[2,16,819,1024]{3,2,1,0:T(8,128)} %fusion.77, bf16[16,2,819,512]{3,2,0,1:T(8,128)(2,1)} %get-tuple-element.15, bf16[2,1024,512]{2,1,0:T(8,128)(2,1)} %param.17), kind=kOutput, calls=%fused_computation.12 | convolution fusion | flops 27534753792 | bytes 189956096 | tf_op jit(solution)/shard_map/secf,edf->secd/dot_general | solution.py:50
  3316.8 559.4 %all-to-all-done.3 = bf16[16,2022,1024]{2,1,0:T(8,128)(2,1)} async-done(((bf16[16,2022,1024]{2,1,0:T(8,128)(2,1)}), bf16[16,2022,1024]{2,1,0:T(8,128)(2,1)}, u32[]{:S(2)}, u32[]{:S(2)}) %all-to-all-start.3) | async-done | bytes 66256928 | tf_op jit(solution)/shard_map/all_to_all | solution.py:83
  3926.2 848.9 %all-reduce.5.cloned.1.call-done = (f32[2,1024,512]{2,1,0:T(8,128)}, f32[2,1024,512]{2,1,0:T(8,128)}, f32[2,512,1024]{2,1,0:T(8,128)}) async-done(((f32[2,1024,512]{2,1,0:T(8,128)}, f32[2,1024,512]{2,1,0:T(8,128)}, f32[2,512,1024]{2,1,0:T(8,128)}), (f32[2,1024,512]{2,1,0:T(8,128)}, f32[2,1024,512]{2,1,0:T(8,128)}, f32[2,512,1024]{2,1,0:T(8,128)})) %all-reduce.5.cloned.1.call-update) | async-done | bytes 12582928 | tf_op jit(solution)/shard_map/psum | solution.py:106
  4786.6 63.2 %fusion.51 = f32[2,1024,512]{2,1,0:T(8,128)} fusion(bf16[16,2,819,1024]{3,0,2,1:T(8,128)(2,1)} %bitcast.225, bf16[16,2,819,512]{3,2,0,1:T(8,128)(2,1)} %get-tuple-element.15, f32[1024,512]{1,0:T(8,128)} %get-tuple-element.24, f32[1024,512]{1,0:T(8,128)} %get-tuple-element.23, f32[2]{0:T(128)S(1)} %get-tuple-element.37, f32[2]{0:T(128)S(1)} %get-tuple-element.38), kind=kOutput, calls=%fused_computation.83 | convolution fusion | flops 27485274112 | bytes 88899600 | tf_op jit(solution)/shard_map/secd,secf->edf/dot_general | solution.py:52
  4849.8 63.6 %fusion.52 = f32[2,1024,512]{2,1,0:T(8,128)} fusion(bf16[16,2,819,1024]{3,0,2,1:T(8,128)(2,1)} %bitcast.226, bf16[16,2,819,512]{3,2,0,1:T(8,128)(2,1)} %get-tuple-element.16, f32[1024,512]{1,0:T(8,128)} %get-tuple-element.26, f32[2]{0:T(128)S(1)} %get-tuple-element.37, f32[1024,512]{1,0:T(8,128)} %get-tuple-element.25, f32[2]{0:T(128)S(1)} %get-tuple-element.38), kind=kOutput, calls=%fused_computation.85 | convolution fusion | flops 27485274112 | bytes 88899600 | tf_op jit(solution)/shard_map/secd,secf->edf/dot_general | solution.py:51
  4913.4 100.5 %fusion.50 = f32[2,512,1024]{2,1,0:T(8,128)} fusion(bf16[16,2,819,512]{3,2,0,1:T(8,128)(2,1)} %get-tuple-element.17, bf16[16,2,819,1024]{3,0,2,1:T(8,128)(2,1)} %bitcast.228, f32[512,1024]{1,0:T(8,128)} %get-tuple-element.22, f32[2]{0:T(128)S(1)} %get-tuple-element.37, f32[512,1024]{1,0:T(8,128)S(1)} %get-tuple-element.21, f32[2]{0:T(128)S(1)} %get-tuple-element.38), kind=kOutput, calls=%fused_computation.81 | convolution fusion | flops 27485274112 | bytes 88899600 | tf_op jit(solution)/shard_map/secf,secd->efd/dot_general | solution.py:53
  5013.9 62.6 %reshape.364 = bf16[32352,1024]{1,0:T(8,128)(2,1)} reshape(bf16[16,2022,1024]{2,1,0:T(8,128)(2,1)} %all-to-all-done.3) | data formatting | bytes 132513792 | tf_op jit(solution)/shard_map/reshape | solution.py:103
  5076.5 225.3 %gather_fusion.4 = bf16[12288,1024]{1,0:T(8,128)(2,1)} fusion(bf16[32352,1024]{1,0:T(8,128)(2,1)} %reshape.364, s32[12288]{0:T(1024)S(1)} %copy-done.3), kind=kCustom, calls=%fused_computation.3.clone | custom fusion | bytes 50380800 | tf_op jit(solution)/shard_map/jit(_take)/gather | solution.py:104
  5301.7 62.7 %reshape.357 = bf16[32352,1024]{1,0:T(8,128)(2,1)} reshape(bf16[16,2022,1024]{2,1,0:T(8,128)(2,1)} %all-to-all-done.1) | data formatting | bytes 132513792 | tf_op jit(solution)/shard_map/reshape | solution.py:96
  5364.5 225.1 %gather_fusion.2 = bf16[12288,1024]{1,0:T(8,128)(2,1)} fusion(bf16[32352,1024]{1,0:T(8,128)(2,1)} %reshape.357, s32[12288]{0:T(1024)S(1)} %copy-done.3), kind=kCustom, calls=%fused_computation.1.clone | custom fusion | bytes 50380800 | tf_op jit(solution)/shard_map/jit(_take)/gather | solution.py:97
  (125 shorter events, 817.2 us)
Async XLA Ops:
  7.2 183.2 %copy-start = (bf16[1536,1024]{1,0:T(8,128)(2,1)S(1)}, bf16[1536,1024]{1,0:T(8,128)(2,1)}, u32[]{:S(2)}) copy-start(bf16[1536,1024]{1,0:T(8,128)(2,1)} %param.12) | copy-start | bytes 9437188
  7.2 33.4 copy-start.2
  40.2 103.1 %copy-start.9 = (s32[12288]{0:T(1024)}, s32[12288]{0:T(1024)S(1)}, u32[]{:S(2)}) copy-start(s32[12288]{0:T(1024)S(1)} %fusion.83) | copy-start | bytes 147460
  144.0 144.1 %copy-start.17 = (s32[12288,1]{0,1:T(1,128)}, s32[12288,1]{0,1:T(1,128)S(1)}, u32[]{:S(2)}) copy-start(s32[12288,1]{0,1:T(1,128)S(1)} %compare_select_fusion.1) | copy-start | bytes 147460
  288.1 140.4 %copy-start.15 = (bf16[1536,8]{0,1:T(8,128)(2,1)S(1)}, bf16[1536,8]{0,1:T(8,128)(2,1)}, u32[]{:S(2)}) copy-start(bf16[1536,8]{0,1:T(8,128)(2,1)} %param.14) | copy-start | bytes 73732
  288.1 226.1 %copy-start.14 = (pred[32352]{0:T(1024)(128)(4,1)S(1)}, pred[32352]{0:T(1024)(128)(4,1)}, u32[]{:S(2)}) copy-start(pred[32352]{0:T(1024)(128)(4,1)} %compare_and_fusion) | copy-start | bytes 97060
  663.0 787.5 %all-to-all-start = ((bf16[16,2022,1024]{2,1,0:T(8,128)(2,1)}), bf16[16,2022,1024]{2,1,0:T(8,128)(2,1)}, u32[]{:S(2)}, u32[]{:S(2)}) async-start(bf16[16,2022,1024]{2,1,0:T(8,128)(2,1)} %reshape.352), calls=%async_computation | async-start | bytes 132644864 | tf_op jit(solution)/shard_map/all_to_all | solution.py:83
  1450.5 1034.4 %all-to-all-start.2 = ((bf16[16,2022,1024]{2,1,0:T(8,128)(2,1)}), bf16[16,2022,1024]{2,1,0:T(8,128)(2,1)}, u32[]{:S(2)}, u32[]{:S(2)}) async-start(bf16[16,2022,1024]{2,1,0:T(8,128)(2,1)} %reshape.359), calls=%async_computation.2 | async-start | bytes 132644864 | tf_op jit(solution)/shard_map/all_to_all | solution.py:83
  1456.5 817.5 %all-reduce.7.cloned.1.call-start = ((), (), s32[]{:S(2)}) async-start(), calls=%async_computation.5 | async-start | bytes 12582912 | tf_op jit(solution)/shard_map/psum | solution.py:76
  2274.0 14.6 copy-start.21
  2302.8 91.2 %copy-start.5 = (bf16[2,1024,512]{2,1,0:T(8,128)(2,1)S(1)}, bf16[2,1024,512]{2,1,0:T(8,128)(2,1)}, u32[]{:S(2)}) copy-start(bf16[2,1024,512]{2,1,0:T(8,128)(2,1)} %param.16) | copy-start | bytes 6291460
  2633.6 112.4 %copy-start.6 = (bf16[2,1024,512]{2,1,0:T(8,128)(2,1)S(1)}, bf16[2,1024,512]{2,1,0:T(8,128)(2,1)}, u32[]{:S(2)}) copy-start(bf16[2,1024,512]{2,1,0:T(8,128)(2,1)} %param.16) | copy-start | bytes 6291460
  2905.6 11.9 copy-start.18
  2941.4 15.5 copy-start.20
  3089.5 786.7 %all-to-all-start.3 = ((bf16[16,2022,1024]{2,1,0:T(8,128)(2,1)}), bf16[16,2022,1024]{2,1,0:T(8,128)(2,1)}, u32[]{:S(2)}, u32[]{:S(2)}) async-start(bf16[16,2022,1024]{2,1,0:T(8,128)(2,1)} %copy.121), calls=%async_computation.3 | async-start | bytes 132644864 | tf_op jit(solution)/shard_map/all_to_all | solution.py:83
  3139.5 48.4 copy-start.19
  3876.2 1425.5 %all-to-all-start.1 = ((bf16[16,2022,1024]{2,1,0:T(8,128)(2,1)}), bf16[16,2022,1024]{2,1,0:T(8,128)(2,1)}, u32[]{:S(2)}, u32[]{:S(2)}) async-start(bf16[16,2022,1024]{2,1,0:T(8,128)(2,1)} %copy.111), calls=%async_computation.1 | async-start | bytes 132644864 | tf_op jit(solution)/shard_map/all_to_all | solution.py:83
  3882.3 892.9 %all-reduce.5.cloned.1.call-start = ((), (), s32[]{:S(2)}) async-start(), calls=%async_computation.4 | async-start | bytes 25165824 | tf_op jit(solution)/shard_map/psum | solution.py:106
  3882.3 26.5 slice-start
  3895.8 13.0 slice-start.1
  4775.1 9.0 copy-start.4
  5013.9 62.6 %copy-start.3 = (s32[12288]{0:T(1024)S(1)}, s32[12288]{0:T(1024)}, u32[]{:S(2)}) copy-start(s32[12288]{0:T(1024)} %broadcast_clamp_fusion) | copy-start | bytes 147460
  5364.5 225.1 %copy-start.8 = (pred[1536,8]{1,0:T(8,128)(4,1)S(1)}, pred[1536,8]{1,0:T(8,128)(4,1)}, u32[]{:S(2)}) copy-start(pred[1536,8]{1,0:T(8,128)(4,1)} %copy.102) | copy-start | bytes 36868
  5608.4 14.7 copy-start.1
  (6 other events, 15.2 us)
Sparse Core Ops, SparseCore 0:
  1465.5 808.4 all-reduce.6
  3920.0 855.1 all-reduce.4
where the time goes:
time: 5650 us; the launch traced here: 5630 us
  waiting for transfers between devices  2770 us (49%)
  local copies, waits for them, and re-layouts  1760 us (31%)
  matrix products  823 us (15%)
  other arithmetic  230 us (4%)
    all_to_all x4, waiting for transfers between devices, exchange(): lax.all_to_all(send_rows.reshape(n_dev, block_rows, model_dim), 'ep', 0, 0)  1280 us
    psum x1, waiting for transfers between devices, local_step(): h_gate, h_up, h_down = lax.psum((h_gate, h_up, h_down), 'ep')  849 us
    psum x1, waiting for transfers between devices, hot_copy(): return lax.psum(jnp.stack([first_copy, second_copy]), 'ep')  647 us
    slice x4, local copies, waits for them, and re-layouts, split_recv(): recv_rows[:, :reg_rows].reshape(n_dev, per_dev, slot_cap, model_dim)  298 us
    gather x1, local copies, waits for them, and re-layouts, local_step(): jnp.take(dx_back, slot_idx, axis=0)  225 us
    gather x1, local copies, waits for them, and re-layouts, local_step(): jnp.take(o_back, slot_idx, axis=0)  225 us
    gather x1, local copies, waits for them, and re-layouts, local_step(): jnp.take(dy_tok, src_tok, axis=0, mode='fill', fill_value=0)  140 us
    dot_general x2, matrix products, expert_backward(): jnp.einsum('secd,efd->secf', d_out, down_w, preferred_element_type=jnp.fl...  136 us
  transfers between devices with their start and end apart: 6, of which 4 were waited for; matrix products, arithmetic and copies ran while one was open for 22% of the time, Pallas kernels for 0%

commit v1 on v0

v1 whole, which is shorter than its diff:
```python
import functools

import jax
import jax.numpy as jnp
from jax import lax
from jax.experimental import pallas as pl
from jax.experimental.pallas import tpu as pltpu
from jax.sharding import PartitionSpec as P


BF = jnp.bfloat16
F32 = jnp.float32
I32 = jnp.int32
TILE = 256
GROUP = 8
KEY_STEP = 4096
EXPERTS = ((4, 0), (8, 1), (12, 0), (12, 1), (8, 0), (4, 1), (0, 0), (0, 1))
NEAR_ORDER = ((0, 0), (0, 1), (8, 0), (4, 1), (4, 0), (8, 1))
ANY = pl.BlockSpec(memory_space=pl.ANY)


def dot_nt(lhs, rhs):
    return lax.dot_general(lhs, rhs, (((1,), (1,)), ((), ())), preferred_element_type=F32)


def dot_tn(lhs, rhs):
    return lax.dot_general(lhs, rhs, (((0,), (0,)), ((), ())), preferred_element_type=F32)


def dot_nn(lhs, rhs):
    return jnp.dot(lhs, rhs, preferred_element_type=F32)


def gather_kernel(lanes, n_src, total, tok, gate, mate_ref, own_ref, x_out, g_out, table, x_stage, g_stage, sems):
    step = pl.program_id(0)

    @pl.when(step == 0)
    def _():
        copies = [pltpu.make_async_copy(ref, table.at[pl.ds(i * n_src, n_src)], sems.at[i]) for i, ref in enumerate((mate_ref, own_ref))]
        for copy in copies:
            copy.start()
        table[2 * n_src] = jnp.zeros_like(table[2 * n_src])
        for copy in copies:
            copy.wait()

    @pl.when(step < total[0])
    def _():
        base = step * TILE

        def body(block, carry):
            row0 = block * GROUP
            for q in range(GROUP):
                pos = base + row0 + q
                both = table[tok[pos]]
                dst = pl.ds(pl.multiple_of((row0 + q) * lanes, lanes), lanes)
                x_stage[dst, :] = both[:lanes].astype(F32)
                g_stage[dst, :] = both[lanes:].astype(F32) * gate[pos]
            return carry

        lax.fori_loop(0, TILE // GROUP, body, 0)
        for c in range(lanes):
            cols = slice(c * 128, (c + 1) * 128)
            x_out[:, cols] = x_stage[pl.ds(c, TILE, stride=lanes), :].astype(BF)
            g_out[:, cols] = g_stage[pl.ds(c, TILE, stride=lanes), :].astype(BF)


def expert_kernel(ff, dim, which, has_init, n_carried, first_tile, n_tiles, x_ref, g_ref, w_ref, *rest):
    init_ref = rest[0] if has_init else None
    o_ref, dx_ref, p_ref, sem = rest[n_carried + int(has_init):]
    step = pl.program_id(0)

    @pl.when(step == 0)
    def _():
        if has_init:
            pltpu.make_async_copy(init_ref, p_ref, sem).start()
        else:
            def clear(i, carry):
                p_ref[pl.ds(pl.multiple_of(i * 64, 64), 64), :] = jnp.zeros((64, p_ref.shape[1]), F32)
                return carry

            lax.fori_loop(0, p_ref.shape[0] // 64, clear, 0)

    @pl.when(step < n_tiles[which])
    def _():
        x_rows = x_ref[...]
        g_rows = g_ref[...]
        gate_w = w_ref[0:dim, :]
        up_w = w_ref[dim:2 * dim, :]
        u_val = dot_nn(x_rows, gate_w)
        v_val = dot_nn(x_rows, up_w)
        sig = jax.nn.sigmoid(u_val)
        act = (u_val * sig * v_val).astype(BF)
        halves = dim // ff
        d_act = None
        for h in range(halves):
            down = w_ref[2 * dim + h * ff:2 * dim + (h + 1) * ff, :]
            o_ref[:, h * ff:(h + 1) * ff] = dot_nn(act, down).astype(BF)
            part = dot_nt(g_rows[:, h * ff:(h + 1) * ff], down)
            d_act = part if d_act is None else d_act + part
        d_u = (d_act * v_val * sig * (1.0 + u_val * (1.0 - sig))).astype(BF)
        d_v = (d_act * u_val * sig).astype(BF)
        dx_ref[...] = (dot_nt(d_u, gate_w) + dot_nt(d_v, up_w)).astype(BF)
        if has_init:
            @pl.when(step == 0)
            def _():
                pltpu.make_async_copy(init_ref, p_ref, sem).wait()
        p_ref[0:dim, :] += dot_tn(x_rows, d_u)
        p_ref[dim:2 * dim, :] += dot_tn(x_rows, d_v)
        for h in range(halves):
            p_ref[2 * dim + h * ff:2 * dim + (h + 1) * ff, :] += dot_tn(act, g_rows[:, h * ff:(h + 1) * ff])


def combine_kernel(lanes, n_src, use_gate, total, tok, gate, rows_ref, mate_out, own_out, acc, stage, sems):
    step = pl.program_id(0)

    @pl.when(step == 0)
    def _():
        def clear(i, carry):
            acc[pl.ds(pl.multiple_of(i * 8, 8), 8)] = jnp.zeros((8, lanes, 128), F32)
            return carry

        lax.fori_loop(0, acc.shape[0] // 8, clear, 0)

    @pl.when(step < total[0])
    def _():
        base = step * TILE
        for c in range(lanes):
            stage[pl.ds(c, TILE, stride=lanes), :] = rows_ref[:, c * 128:(c + 1) * 128].astype(F32)

        def body(block, carry):
            row0 = block * GROUP
            dests, sums = [], []
            for q in range(GROUP):
                pos = base + row0 + q
                t = tok[pos]
                value = stage[pl.ds(pl.multiple_of((row0 + q) * lanes, lanes), lanes), :]
                if use_gate:
                    value = value * gate[pos]
                dests.append(t)
                sums.append(acc[t] + value)
            for t, total_row in zip(dests, sums):
                acc[t] = total_row
            return carry

        lax.fori_loop(0, TILE // GROUP, body, 0)

    @pl.when(step == pl.num_programs(0) - 1)
    def _():
        copies = [pltpu.make_async_copy(acc.at[pl.ds(i * n_src, n_src)], ref, sems.at[i]) for i, ref in enumerate((mate_out, own_out))]
        for copy in copies:
            copy.start()
        for copy in copies:
            copy.wait()


def solution(mesh):
    n_dev = mesh.shape['ep']

    def permute(value, mask):
        return lax.ppermute(value, 'ep', [(i, i ^ mask) for i in range(n_dev)])

    def layer(x_tok, route_idx, gates, dy_tok, w_gate, w_up, w_down):
        tok_loc, top_k = route_idx.shape
        dim, ff = w_gate.shape[1], w_gate.shape[2]
        experts = w_gate.shape[0] * n_dev
        lanes = dim // 128
        n_exp = len(EXPERTS)
        slot_cap = max(2 * tok_loc * top_k // (experts - 2), tok_loc // 2)
        max_tiles = -(-2 * slot_cap // TILE)
        n_slots = n_exp * max_tiles
        list_len = n_slots * TILE
        n_half = 2 * tok_loc
        me = lax.axis_index('ep')

        routing = jnp.concatenate([route_idx.T.astype(F32), gates.T.astype(F32)], axis=0)
        rt_mate = permute(routing, 1)
        rt_xp = permute(routing, 2)
        rt_xpm = permute(rt_xp, 1)
        pack_w = jnp.concatenate([w_gate, w_up, w_down[:, :, :ff], w_down[:, :, ff:]], axis=1)
        wts = {(0, 0): pack_w[0], (0, 1): pack_w[1]}
        wts[(8, 0)] = permute(wts[(0, 0)], 8)
        wts[(4, 1)] = permute(wts[(0, 1)], 4)
        wts[(4, 0)] = permute(wts[(0, 0)], 4)
        wts[(8, 1)] = permute(wts[(0, 1)], 8)
        wts[(12, 0)] = permute(wts[(8, 0)], 4)
        wts[(12, 1)] = permute(wts[(4, 1)], 8)
        xd_own = jnp.concatenate([x_tok.reshape(tok_loc, lanes, 128), dy_tok.reshape(tok_loc, lanes, 128)], axis=1)
        xd_xp = permute(xd_own, 2)
        xd_mate = permute(xd_own, 1)
        xd_xpm = permute(xd_xp, 1)

        def plan(rt_pair):
            route = jnp.stack([r[:top_k] for r in rt_pair], axis=1).astype(I32)
            gate = jnp.stack([r[top_k:] for r in rt_pair], axis=1)
            place = (route // 2) ^ me
            slot = jnp.full_like(route, n_exp)
            for j, (mask, which) in enumerate(EXPERTS):
                slot = jnp.where((place == mask) & (route % 2 == which), j, slot)
            token = lax.broadcasted_iota(I32, route.shape, 1) * tok_loc + lax.broadcasted_iota(I32, route.shape, 2)
            key = slot * KEY_STEP + token
            counts = jnp.stack([jnp.sum((slot == j).astype(I32)) for j in range(n_exp)])
            n_tiles = jnp.maximum(1, (counts + TILE - 1) // TILE)
            need = n_tiles * TILE - counts
            pad_key = jnp.where(jnp.arange(TILE)[None, :] < need[:, None], jnp.arange(n_exp)[:, None] * KEY_STEP + n_half, n_exp * KEY_STEP)
            keys = jnp.concatenate([key.reshape(-1), pad_key.reshape(-1)])
            vals = jnp.concatenate([gate.reshape(-1), jnp.zeros((n_exp * TILE,), F32)])
            keys, vals = lax.sort((keys, vals), num_keys=1)
            tile_ends = jnp.cumsum(n_tiles)
            return (tile_ends[n_exp - 1:], keys[:list_len] & (KEY_STEP - 1), vals[:list_len]), (tile_ends - n_tiles, n_tiles)

        row_shape = jax.ShapeDtypeStruct((list_len, dim), BF)
        tile_spec = pl.BlockSpec((TILE, dim), lambda i, n, *s: (jnp.minimum(i, n[0] - 1), 0))

        def gather(lists, mate, own):
            return pl.pallas_call(
                functools.partial(gather_kernel, lanes, tok_loc),
                grid_spec=pltpu.PrefetchScalarGridSpec(
                    num_scalar_prefetch=3, grid=(n_slots,), in_specs=[ANY, ANY], out_specs=[tile_spec, tile_spec],
                    scratch_shapes=[pltpu.VMEM((n_half + 8, 2 * lanes, 128), BF), pltpu.VMEM((TILE * lanes, 128), F32), pltpu.VMEM((TILE * lanes, 128), F32), pltpu.SemaphoreType.DMA((2,))]),
                out_shape=[row_shape, row_shape],
                compiler_params=pltpu.CompilerParams(dimension_semantics=('arbitrary',), vmem_limit_bytes=48 * 1024 * 1024),
                name='gather_rows',
            )(*lists, mate, own)

        def expert(key, tiles, rows, carried, init):
            j = EXPERTS.index(key)
            blk = pl.BlockSpec((TILE, dim), lambda i, first, n: (first[j] + jnp.minimum(i, n[j] - 1), 0))
            pack = pl.BlockSpec((3 * dim, ff), lambda i, first, n: (0, 0))
            extra = ([] if init is None else [init]) + list(carried)
            first_alias = 5 + (init is not None)
            return pl.pallas_call(
                functools.partial(expert_kernel, ff, dim, j, init is not None, len(carried)),
                grid_spec=pltpu.PrefetchScalarGridSpec(
                    num_scalar_prefetch=2, grid=(max_tiles,), in_specs=[blk, blk, pack] + [ANY] * len(extra), out_specs=[blk, blk, pack],
                    scratch_shapes=[pltpu.SemaphoreType.DMA]),
                out_shape=[row_shape, row_shape, jax.ShapeDtypeStruct((3 * dim, ff), F32)],
                input_output_aliases={first_alias: 0, first_alias + 1: 1} if carried else {},
                compiler_params=pltpu.CompilerParams(dimension_semantics=('arbitrary',), vmem_limit_bytes=48 * 1024 * 1024),
                name='expert_step',
            )(*tiles, *rows, wts[key], *extra)

        def combine(lists, rows, use_gate):
            block = jax.ShapeDtypeStruct((tok_loc, lanes, 128), F32)
            return pl.pallas_call(
                functools.partial(combine_kernel, lanes, tok_loc, use_gate),
                grid_spec=pltpu.PrefetchScalarGridSpec(
                    num_scalar_prefetch=3, grid=(n_slots,), in_specs=[tile_spec], out_specs=[ANY, ANY],
                    scratch_shapes=[pltpu.VMEM((n_half + 8, lanes, 128), F32), pltpu.VMEM((TILE * lanes, 128), F32), pltpu.SemaphoreType.DMA((2,))]),
                out_shape=[block, block],
                compiler_params=pltpu.CompilerParams(dimension_semantics=('arbitrary',), vmem_limit_bytes=48 * 1024 * 1024),
                name='combine_rows',
            )(*lists, rows)

        lists0, tiles0 = plan((rt_mate, routing))
        lists1, tiles1 = plan((rt_xpm, rt_xp))
        rows0 = gather(lists0, xd_mate, xd_own)
        out0, out1, part, grads = (), (), {}, {}
        for key in NEAR_ORDER:
            *out0, part[key] = expert(key, tiles0, rows0, out0, None)
        rows1 = gather(lists1, xd_xpm, xd_xp)
        for key in EXPERTS:
            if key not in part:
                *out0, part[key] = expert(key, tiles0, rows0, out0, None)
            *out1, grads[key] = expert(key, tiles1, rows1, out1, part[key])

        def settle_rows(which, use_gate):
            mate1, own1 = combine(lists1, out1[which], use_gate)
            to_x = own1 + permute(mate1, 1)
            mate0, own0 = combine(lists0, out0[which], use_gate)
            total = own0 + permute(mate0, 1) + permute(to_x, 2)
            return total.astype(BF).reshape(tok_loc, dim)

        y_tok = settle_rows(0, True)
        dx_tok = settle_rows(1, False)

        g_a = grads[(0, 0)] + permute(grads[(4, 0)], 4)
        g_a = g_a + permute(grads[(8, 0)] + permute(grads[(12, 0)], 4), 8)
        g_b = grads[(0, 1)] + permute(grads[(8, 1)], 8)
        g_b = g_b + permute(grads[(4, 1)] + permute(grads[(12, 1)], 8), 4)
        both = jnp.stack([g_a, g_b])
        d_down = jnp.concatenate([both[:, 2 * dim:2 * dim + ff], both[:, 2 * dim + ff:]], axis=2)
        return y_tok, dx_tok, both[:, :dim], both[:, dim:2 * dim], d_down

    return jax.shard_map(layer, mesh=mesh, in_specs=(P('ep'),) * 7, out_specs=(P('ep'),) * 5, check_vma=False)
```

time: 5650 us -> 1080 us (0.19)
  waiting for transfers between devices: 2770 us -> 360 us
  local copies, waits for them, and re-layouts: 1760 us -> 49 us
  matrix products: 823 us -> 0 us
  Pallas kernels: 0 us -> 490 us
  other arithmetic: 230 us -> 128 us
    psum x2 -> x0, waiting for transfers between devices: 1500 us -> none  [the longest x1 849 us: local_step(): h_gate, h_up, h_down = lax.psum((h_gate, h_up, h_down), 'ep')]
    all_to_all x4 -> x0, waiting for transfers between devices: 1280 us -> none  [exchange(): lax.all_to_all(send_rows.reshape(n_dev, block_rows, model_dim), 'ep', 0, 0)]
    dot_general x19 -> x0, matrix products: 823 us -> none  [the longest x2 136 us: expert_backward(): jnp.einsum('secd,efd->secf', d_out, down_w, preferred_element_type=jnp.fl...]
    gather x7 -> x0, local copies, waits for them, and re-layouts: 792 us -> none  [the longest x1 225 us: local_step(): jnp.take(dx_back, slot_idx, axis=0)]
    pallas_call x0 -> x22, Pallas kernels: none -> 490 us  [the longest x16 267 us: expert(): pl.pallas_call(functools.partial(expert_kernel, ff, dim, j, init is not N...]
    ppermute x0 -> x24, waiting for transfers between devices: none -> 360 us  [permute(): return lax.ppermute(value, 'ep', [(i, i ^ mask) for i in range(n_dev)])]
    slice x7 -> x5, local copies, waits for them, and re-layouts: 324 us -> 3.08 us  [the longest x2 1.65 us: plan(): vals[:list_len]]
    reshape x8 -> x2, local copies, waits for them, and re-layouts: 294 us -> 0.16 us  [plan(): vals = jnp.concatenate([gate.reshape(-1), jnp.zeros((n_exp * TILE,), F32)])]
  transfers between devices with their start and end apart: 6 -> 24, of which waited for: 4 -> 6; matrix products, arithmetic and copies ran while one was open for 22% -> 14% of each run, Pallas kernels for 0% -> 26%
where the time goes in v1:
time: 1080 us; the launch traced here: 1070 us
  Pallas kernels  490 us (45%)
  waiting for transfers between devices  360 us (33%)
  other arithmetic  128 us (12%)
  local copies, waits for them, and re-layouts  49 us (5%)
  starting transfers between devices  44.6 us (4%)
    ppermute x24, waiting for transfers between devices, permute(): return lax.ppermute(value, 'ep', [(i, i ^ mask) for i in range(n_dev)])  360 us
    pallas_call x16, Pallas kernels, expert(): pl.pallas_call(functools.partial(expert_kernel, ff, dim, j, init is not N...  267 us
    pallas_call x4, Pallas kernels, combine(): pl.pallas_call(functools.partial(combine_kernel, lanes, tok_loc, use_gate...  146 us
    pallas_call x2, Pallas kernels, gather(): pl.pallas_call(functools.partial(gather_kernel, lanes, tok_loc), grid_spe...  77.9 us
    ppermute x24, starting transfers between devices, permute(): return lax.ppermute(value, 'ep', [(i, i ^ mask) for i in range(n_dev)])  44.6 us
    sort x2, other arithmetic, plan(): keys, vals = lax.sort((keys, vals), num_keys=1)  36.7 us
    another operation x4, other arithmetic, layer(): both = jnp.stack([g_a, g_b])  25.5 us
  transfers between devices with their start and end apart: 24, of which 6 were waited for; matrix products, arithmetic and copies ran while one was open for 14% of the time, Pallas kernels for 26%

profile of v1, /device:TPU:0, one launch (start us, length us, event | category | flops | bytes accessed | tf_op | source)
XLA Modules:
  0.0 1072.6 jit_solution(15204875807489144028)
XLA Ops:
  28.6 118.6 %collective-permute-done.11.own_ref = bf16[1536,16,128]{2,1,0:T(8,128)(2,1)} collective-permute-done((bf16[1536,16,128]{2,1,0:T(8,128)(2,1)}, bf16[1536,16,128]{2,1,0:T(8,128)(2,1)}, u32[]{:S(2)}, u32[]{:S(2)}) %collective-permute-start.11) | collective-permute-done | bytes 6291488 | tf_op jit(solution)/shard_map/ppermute | solution.py:160
  189.2 18.3 %sort.47 = (s32[26624]{0:T(1024)}, f32[26624]{0:T(1024)}, s32[26624]{0:T(1024)}) sort(s32[26624]{0:T(1024)} %pad_add_fusion.1, f32[26624]{0:T(1024)S(1)} %concatenate.56, s32[26624]{0:T(1024)} %iota.50), dimensions={0}, to_apply=%region_19.20 | sort | flops 399360 | bytes 638976 | tf_op jit(solution)/shard_map/sort | solution.py:207
  209.9 18.4 %sort.46 = (s32[26624]{0:T(1024)}, f32[26624]{0:T(1024)}, s32[26624]{0:T(1024)}) sort(s32[26624]{0:T(1024)S(1)} %pad_add_fusion, f32[26624]{0:T(1024)S(1)} %concatenate.52, s32[26624]{0:T(1024)} %iota.49), dimensions={0}, to_apply=%region_9.10 | sort | flops 399360 | bytes 638976 | tf_op jit(solution)/shard_map/sort | solution.py:207
  230.8 38.5 %gather_rows.2 = (bf16[14336,1024]{1,0:T(8,128)(2,1)}, bf16[14336,1024]{1,0:T(8,128)(2,1)}) custom-call(s32[1]{0:T(128)} %bitcast.12.total, s32[14336]{0:T(1024)S(1)} %slice_and_fusion.1.tok, f32[14336]{0:T(1024)S(1)} %slice.71.gate, bf16[1536,16,128]{2,1,0:T(8,128)(2,1)} %collective-permute-done.1.mate_ref, ...), custom_call_target="tpu_custom_call" | custom-call | tf_op jit(solution)/shard_map/gather_rows/pallas_call | solution.py:215
  269.3 20.1 %expert_step.16 = (bf16[14336,1024]{1,0:T(8,128)(2,1)}, bf16[14336,1024]{1,0:T(8,128)(2,1)}, f32[3072,512]{1,0:T(8,128)}) custom-call(s32[8]{0:T(128)S(1)} %bitcast_subtract_fusion.1.first_tile, s32[8]{0:T(128)S(1)} %get-tuple-element.154.n_tiles, bf16[14336,1024]{1,0:T(8,128)(2,1)} %get-tuple-element.75.x_ref, bf16[14336,1024]{1,0:T(8,128)(2,1)} %get-tuple-element.76.g_ref, ...), custom_call_target="tpu_custom_call" | custom-call | tf_op jit(solution)/shard_map/expert_step/pallas_call | solution.py:231
  304.9 15.6 %expert_step.18 = (bf16[14336,1024]{1,0:T(8,128)(2,1)}, bf16[14336,1024]{1,0:T(8,128)(2,1)}, f32[3072,512]{1,0:T(8,128)}) custom-call(s32[8]{0:T(128)S(1)} %bitcast_subtract_fusion.1.first_tile, s32[8]{0:T(128)S(1)} %get-tuple-element.154.n_tiles, bf16[14336,1024]{1,0:T(8,128)(2,1)} %get-tuple-element.75.x_ref, ...), custom_call_target="tpu_custom_call", output_to_operand_aliasing={{0}: (5, {}), {1}: (6, {})} | custom-call | tf_op jit(solution)/shard_map/expert_step/pallas_call | solution.py:231
  366.7 15.6 %expert_step.22 = (bf16[14336,1024]{1,0:T(8,128)(2,1)}, bf16[14336,1024]{1,0:T(8,128)(2,1)}, f32[3072,512]{1,0:T(8,128)}) custom-call(s32[8]{0:T(128)S(1)} %bitcast_subtract_fusion.1.first_tile, s32[8]{0:T(128)S(1)} %get-tuple-element.154.n_tiles, bf16[14336,1024]{1,0:T(8,128)(2,1)} %get-tuple-element.75.x_ref, ...), custom_call_target="tpu_custom_call", output_to_operand_aliasing={{0}: (5, {}), {1}: (6, {})} | custom-call | tf_op jit(solution)/shard_map/expert_step/pallas_call | solution.py:231
  382.3 15.5 %expert_step.23 = (bf16[14336,1024]{1,0:T(8,128)(2,1)}, bf16[14336,1024]{1,0:T(8,128)(2,1)}, f32[3072,512]{1,0:T(8,128)}) custom-call(s32[8]{0:T(128)S(1)} %bitcast_subtract_fusion.1.first_tile, s32[8]{0:T(128)S(1)} %get-tuple-element.154.n_tiles, bf16[14336,1024]{1,0:T(8,128)(2,1)} %get-tuple-element.75.x_ref, ...), custom_call_target="tpu_custom_call", output_to_operand_aliasing={{0}: (5, {}), {1}: (6, {})} | custom-call | tf_op jit(solution)/shard_map/expert_step/pallas_call | solution.py:231
  397.8 39.5 %gather_rows.3 = (bf16[14336,1024]{1,0:T(8,128)(2,1)}, bf16[14336,1024]{1,0:T(8,128)(2,1)}) custom-call(s32[1]{0:T(128)} %bitcast.36.total, s32[14336]{0:T(1024)S(1)} %slice_and_fusion.tok, f32[14336]{0:T(1024)S(1)} %slice.83.gate, bf16[1536,16,128]{2,1,0:T(8,128)(2,1)} %collective-permute-done.12.mate_ref, ...), custom_call_target="tpu_custom_call" | custom-call | tf_op jit(solution)/shard_map/gather_rows/pallas_call | solution.py:215
  437.3 16.2 %expert_step.24 = (bf16[14336,1024]{1,0:T(8,128)(2,1)}, bf16[14336,1024]{1,0:T(8,128)(2,1)}, f32[3072,512]{1,0:T(8,128)}) custom-call(s32[8]{0:T(128)S(1)} %get-tuple-element.155.first_tile, s32[8]{0:T(128)S(1)} %copy-done.5, bf16[14336,1024]{1,0:T(8,128)(2,1)} %get-tuple-element.96.x_ref, bf16[14336,1024]{1,0:T(8,128)(2,1)} %get-tuple-element.97.g_ref, ...), custom_call_target="tpu_custom_call" | custom-call | tf_op jit(solution)/shard_map/expert_step/pallas_call | solution.py:231
  453.5 16.1 %expert_step.25 = (bf16[14336,1024]{1,0:T(8,128)(2,1)}, bf16[14336,1024]{1,0:T(8,128)(2,1)}, f32[3072,512]{1,0:T(8,128)}) custom-call(s32[8]{0:T(128)S(1)} %get-tuple-element.155.first_tile, s32[8]{0:T(128)S(1)} %copy-done.5, bf16[14336,1024]{1,0:T(8,128)(2,1)} %get-tuple-element.96.x_ref, ...), custom_call_target="tpu_custom_call", output_to_operand_aliasing={{0}: (6, {}), {1}: (7, {})} | custom-call | tf_op jit(solution)/shard_map/expert_step/pallas_call | solution.py:231
  469.7 16.5 %expert_step.26 = (bf16[14336,1024]{1,0:T(8,128)(2,1)}, bf16[14336,1024]{1,0:T(8,128)(2,1)}, f32[3072,512]{1,0:T(8,128)}) custom-call(s32[8]{0:T(128)S(1)} %get-tuple-element.155.first_tile, s32[8]{0:T(128)S(1)} %copy-done.5, bf16[14336,1024]{1,0:T(8,128)(2,1)} %get-tuple-element.96.x_ref, ...), custom_call_target="tpu_custom_call", output_to_operand_aliasing={{0}: (6, {}), {1}: (7, {})} | custom-call | tf_op jit(solution)/shard_map/expert_step/pallas_call | solution.py:231
  486.2 16.1 %expert_step.27 = (bf16[14336,1024]{1,0:T(8,128)(2,1)}, bf16[14336,1024]{1,0:T(8,128)(2,1)}, f32[3072,512]{1,0:T(8,128)}) custom-call(s32[8]{0:T(128)S(1)} %get-tuple-element.155.first_tile, s32[8]{0:T(128)S(1)} %copy-done.5, bf16[14336,1024]{1,0:T(8,128)(2,1)} %get-tuple-element.96.x_ref, ...), custom_call_target="tpu_custom_call", output_to_operand_aliasing={{0}: (6, {}), {1}: (7, {})} | custom-call | tf_op jit(solution)/shard_map/expert_step/pallas_call | solution.py:231
  502.4 22.5 %expert_step.28 = (bf16[14336,1024]{1,0:T(8,128)(2,1)}, bf16[14336,1024]{1,0:T(8,128)(2,1)}, f32[3072,512]{1,0:T(8,128)}) custom-call(s32[8]{0:T(128)S(1)} %get-tuple-element.155.first_tile, s32[8]{0:T(128)S(1)} %copy-done.5, bf16[14336,1024]{1,0:T(8,128)(2,1)} %get-tuple-element.96.x_ref, ...), custom_call_target="tpu_custom_call", output_to_operand_aliasing={{0}: (6, {}), {1}: (7, {})} | custom-call | tf_op jit(solution)/shard_map/expert_step/pallas_call | solution.py:231
  524.9 16.1 %expert_step.29 = (bf16[14336,1024]{1,0:T(8,128)(2,1)}, bf16[14336,1024]{1,0:T(8,128)(2,1)}, f32[3072,512]{1,0:T(8,128)}) custom-call(s32[8]{0:T(128)S(1)} %get-tuple-element.155.first_tile, s32[8]{0:T(128)S(1)} %copy-done.5, bf16[14336,1024]{1,0:T(8,128)(2,1)} %get-tuple-element.96.x_ref, ...), custom_call_target="tpu_custom_call", output_to_operand_aliasing={{0}: (6, {}), {1}: (7, {})} | custom-call | tf_op jit(solution)/shard_map/expert_step/pallas_call | solution.py:231
  541.0 18.5 %expert_step.30 = (bf16[14336,1024]{1,0:T(8,128)(2,1)}, bf16[14336,1024]{1,0:T(8,128)(2,1)}, f32[3072,512]{1,0:T(8,128)}) custom-call(s32[8]{0:T(128)S(1)} %get-tuple-element.155.first_tile, s32[8]{0:T(128)S(1)} %copy-done.5, bf16[14336,1024]{1,0:T(8,128)(2,1)} %get-tuple-element.96.x_ref, ...), custom_call_target="tpu_custom_call", output_to_operand_aliasing={{0}: (6, {}), {1}: (7, {})} | custom-call | tf_op jit(solution)/shard_map/expert_step/pallas_call | solution.py:231
  559.5 16.2 %expert_step.31 = (bf16[14336,1024]{1,0:T(8,128)(2,1)}, bf16[14336,1024]{1,0:T(8,128)(2,1)}, f32[3072,512]{1,0:T(8,128)}) custom-call(s32[8]{0:T(128)S(1)} %get-tuple-element.155.first_tile, s32[8]{0:T(128)S(1)} %copy-done.5, bf16[14336,1024]{1,0:T(8,128)(2,1)} %get-tuple-element.96.x_ref, ...), custom_call_target="tpu_custom_call", output_to_operand_aliasing={{0}: (6, {}), {1}: (7, {})} | custom-call | tf_op jit(solution)/shard_map/expert_step/pallas_call | solution.py:231
  575.7 37.1 %combine_rows.5 = (f32[1536,8,128]{2,1,0:T(8,128)}, f32[1536,8,128]{2,1,0:T(8,128)}) custom-call(s32[1]{0:T(128)} %bitcast.36.total, s32[14336]{0:T(1024)S(1)} %slice_and_fusion.tok, f32[14336]{0:T(1024)S(1)} %slice.83.gate, bf16[14336,1024]{1,0:T(8,128)(2,1)} %get-tuple-element.120.rows_ref), custom_call_target="tpu_custom_call" | custom-call | tf_op jit(solution)/shard_map/combine_rows/pallas_call | solution.py:244
  627.7 36.3 %combine_rows.4 = (f32[1536,8,128]{2,1,0:T(8,128)}, f32[1536,8,128]{2,1,0:T(8,128)}) custom-call(s32[1]{0:T(128)} %bitcast.12.total, s32[14336]{0:T(1024)S(1)} %copy-done.3, f32[14336]{0:T(1024)S(1)} %copy-done.1, bf16[14336,1024]{1,0:T(8,128)(2,1)} %get-tuple-element.91.rows_ref), custom_call_target="tpu_custom_call" | custom-call | tf_op jit(solution)/shard_map/combine_rows/pallas_call | solution.py:244
  664.1 36.4 %combine_rows.7 = (f32[1536,8,128]{2,1,0:T(8,128)}, f32[1536,8,128]{2,1,0:T(8,128)}) custom-call(s32[1]{0:T(128)} %bitcast.36.total, s32[14336]{0:T(1024)S(1)} %slice_and_fusion.tok, f32[14336]{0:T(1024)S(1)} %slice.83.gate, bf16[14336,1024]{1,0:T(8,128)(2,1)} %get-tuple-element.126.rows_ref), custom_call_target="tpu_custom_call" | custom-call | tf_op jit(solution)/shard_map/combine_rows/pallas_call | solution.py:244
  711.2 40.4 %collective-permute-done.22 = f32[3072,512]{1,0:T(8,128)} collective-permute-done((f32[3072,512]{1,0:T(8,128)}, f32[3072,512]{1,0:T(8,128)}, u32[]{:S(2)}, u32[]{:S(2)}) %collective-permute-start.22) | collective-permute-done | bytes 6291488 | tf_op jit(solution)/shard_map/ppermute | solution.py:160
  782.6 35.8 %combine_rows.6 = (f32[1536,8,128]{2,1,0:T(8,128)}, f32[1536,8,128]{2,1,0:T(8,128)}) custom-call(s32[1]{0:T(128)} %bitcast.12.total, s32[14336]{0:T(1024)S(1)} %copy-done.3, f32[14336]{0:T(1024)S(1)} %copy-done.1, bf16[14336,1024]{1,0:T(8,128)(2,1)} %get-tuple-element.123.rows_ref), custom_call_target="tpu_custom_call" | custom-call | tf_op jit(solution)/shard_map/combine_rows/pallas_call | solution.py:244
  826.3 60.1 %collective-permute-done.21 = f32[3072,512]{1,0:T(8,128)} collective-permute-done((f32[3072,512]{1,0:T(8,128)}, f32[3072,512]{1,0:T(8,128)}, u32[]{:S(2)}, u32[]{:S(2)}) %collective-permute-start.21) | collective-permute-done | bytes 6291488 | tf_op jit(solution)/shard_map/ppermute | solution.py:160
  918.8 125.0 %collective-permute-done.18 = f32[3072,512]{1,0:T(8,128)} collective-permute-done((f32[3072,512]{1,0:T(8,128)}, f32[3072,512]{1,0:T(8,128)}, u32[]{:S(2)}, u32[]{:S(2)}) %collective-permute-start.18) | collective-permute-done | bytes 6291488 | tf_op jit(solution)/shard_map/ppermute | solution.py:160
  (162 shorter events, 261.6 us)
Async XLA Ops:
  8.1 139.0 %collective-permute-start.11 = (bf16[1536,16,128]{2,1,0:T(8,128)(2,1)}, bf16[1536,16,128]{2,1,0:T(8,128)(2,1)}, u32[]{:S(2)}, u32[]{:S(2)}) collective-permute-start(bf16[1536,16,128]{2,1,0:T(8,128)(2,1)} %constant_dynamic-update-slice_fusion.own_ref), channel_id=1, source_target_pairs={{0,2},{1,3},{2,0},{3,1},{4,6},{5,7},{6,4},{7,5},{8,10},{9,11},{10,... | collective-permute-start | bytes 18874376 | tf_op jit(solution)/shard_map/ppermute | solution.py:160
  11.3 172.2 %collective-permute-start.1 = (bf16[1536,16,128]{2,1,0:T(8,128)(2,1)}, bf16[1536,16,128]{2,1,0:T(8,128)(2,1)}, u32[]{:S(2)}, u32[]{:S(2)}) collective-permute-start(bf16[1536,16,128]{2,1,0:T(8,128)(2,1)} %constant_dynamic-update-slice_fusion.own_ref), channel_id=1, source_target_pairs={{0,1},{1,0},{2,3},{3,2},{4,5},{5,4},{6,7},{7,6},{8,9},{9,8},{10,11... | collective-permute-start | bytes 18874376 | tf_op jit(solution)/shard_map/ppermute | solution.py:160
  11.4 136.6 %collective-permute-start = (f32[16,1536]{1,0:T(8,128)S(1)}, f32[16,1536]{1,0:T(8,128)}, u32[]{:S(2)}, u32[]{:S(2)}) collective-permute-start(f32[16,1536]{1,0:T(8,128)S(1)} %pad_maximum_fusion.2), channel_id=1, source_target_pairs={{0,1},{1,0},{2,3},{3,2},{4,5},{5,4},{6,7},{7,6},{8,9},{9,8},{10,11... | collective-permute-start | bytes 294920 | tf_op jit(solution)/shard_map/ppermute | solution.py:160
  25.5 155.9 %collective-permute-start.4 = (bf16[3072,512]{1,0:T(8,128)(2,1)S(1)}, bf16[3072,512]{1,0:T(8,128)(2,1)}, u32[]{:S(2)}, u32[]{:S(2)}) collective-permute-start(bf16[3072,512]{1,0:T(8,128)(2,1)S(1)} %get-tuple-element.159.w_ref), channel_id=1, source_target_pairs={{0,8},{1,9},{2,10},{3,11},{4,12},{5,13},{6,14},{7,15},{8,0},{9,1},... | collective-permute-start | bytes 9437192 | tf_op jit(solution)/shard_map/ppermute | solution.py:160
  27.1 156.0 %collective-permute-start.2 = (bf16[3072,512]{1,0:T(8,128)(2,1)}, bf16[3072,512]{1,0:T(8,128)(2,1)}, u32[]{:S(2)}, u32[]{:S(2)}) collective-permute-start(bf16[3072,512]{1,0:T(8,128)(2,1)} %get-tuple-element.160.w_ref), channel_id=1, source_target_pairs={{0,4},{1,5},{2,6},{3,7},{4,0},{5,1},{6,2},{7,3},{8,12},{9,13},{10,... | collective-permute-start | bytes 9437192 | tf_op jit(solution)/shard_map/ppermute | solution.py:160
  147.2 250.6 %collective-permute-start.12 = (bf16[1536,16,128]{2,1,0:T(8,128)(2,1)}, bf16[1536,16,128]{2,1,0:T(8,128)(2,1)}, u32[]{:S(2)}, u32[]{:S(2)}) collective-permute-start(bf16[1536,16,128]{2,1,0:T(8,128)(2,1)} %collective-permute-done.11.own_ref), channel_id=1, source_target_pairs={{0,1},{1,0},{2,3},{3,2},{4,5},{5,4},{6,7},{7,6},{8,9},{9,8},{10,11... | collective-permute-start | bytes 18874376 | tf_op jit(solution)/shard_map/ppermute | solution.py:160
  148.0 14.1 %collective-permute-start.9 = (f32[16,1536]{1,0:T(8,128)S(1)}, f32[16,1536]{1,0:T(8,128)S(1)}, u32[]{:S(2)}, u32[]{:S(2)}) collective-permute-start(f32[16,1536]{1,0:T(8,128)S(1)} %pad_maximum_fusion.2), channel_id=1, source_target_pairs={{0,2},{1,3},{2,0},{3,1},{4,6},{5,7},{6,4},{7,5},{8,10},{9,11},{10,... | collective-permute-start | bytes 294920 | tf_op jit(solution)/shard_map/ppermute | solution.py:160
  162.0 3.1 collective-permute-start.10
  165.2 170.8 %collective-permute-start.7 = (bf16[3072,512]{1,0:T(8,128)(2,1)S(1)}, bf16[3072,512]{1,0:T(8,128)(2,1)}, u32[]{:S(2)}, u32[]{:S(2)}) collective-permute-start(bf16[3072,512]{1,0:T(8,128)(2,1)S(1)} %get-tuple-element.159.w_ref), channel_id=1, source_target_pairs={{0,4},{1,5},{2,6},{3,7},{4,0},{5,1},{6,2},{7,3},{8,12},{9,13},{10,... | collective-permute-start | bytes 9437192 | tf_op jit(solution)/shard_map/ppermute | solution.py:160
  181.4 169.9 %collective-permute-start.6 = (bf16[3072,512]{1,0:T(8,128)(2,1)}, bf16[3072,512]{1,0:T(8,128)(2,1)}, u32[]{:S(2)}, u32[]{:S(2)}) collective-permute-start(bf16[3072,512]{1,0:T(8,128)(2,1)} %get-tuple-element.160.w_ref), channel_id=1, source_target_pairs={{0,8},{1,9},{2,10},{3,11},{4,12},{5,13},{6,14},{7,15},{8,0},{9,1},... | collective-permute-start | bytes 9437192 | tf_op jit(solution)/shard_map/ppermute | solution.py:160
  183.0 183.7 %collective-permute-start.5 = (bf16[3072,512]{1,0:T(8,128)(2,1)}, bf16[3072,512]{1,0:T(8,128)(2,1)}, u32[]{:S(2)}, u32[]{:S(2)}) collective-permute-start(bf16[3072,512]{1,0:T(8,128)(2,1)} %collective-permute-done.4.w_ref), channel_id=1, source_target_pairs={{0,4},{1,5},{2,6},{3,7},{4,0},{5,1},{6,2},{7,3},{8,12},{9,13},{10,... | collective-permute-start | bytes 9437192 | tf_op jit(solution)/shard_map/ppermute | solution.py:160
  183.5 198.8 %collective-permute-start.3 = (bf16[3072,512]{1,0:T(8,128)(2,1)}, bf16[3072,512]{1,0:T(8,128)(2,1)}, u32[]{:S(2)}, u32[]{:S(2)}) collective-permute-start(bf16[3072,512]{1,0:T(8,128)(2,1)} %collective-permute-done.2.w_ref), channel_id=1, source_target_pairs={{0,8},{1,9},{2,10},{3,11},{4,12},{5,13},{6,14},{7,15},{8,0},{9,1},... | collective-permute-start | bytes 9437192 | tf_op jit(solution)/shard_map/ppermute | solution.py:160
  612.8 87.7 %collective-permute-start.13 = (f32[1536,8,128]{2,1,0:T(8,128)}, f32[1536,8,128]{2,1,0:T(8,128)S(1)}, u32[]{:S(2)}, u32[]{:S(2)}) collective-permute-start(f32[1536,8,128]{2,1,0:T(8,128)} %get-tuple-element.122), channel_id=1, source_target_pairs={{0,1},{1,0},{2,3},{3,2},{4,5},{5,4},{6,7},{7,6},{8,9},{9,8},{10,11... | collective-permute-start | bytes 18874376 | tf_op jit(solution)/shard_map/ppermute | solution.py:160
  612.9 138.7 %collective-permute-start.22 = (f32[3072,512]{1,0:T(8,128)}, f32[3072,512]{1,0:T(8,128)}, u32[]{:S(2)}, u32[]{:S(2)}) collective-permute-start(f32[3072,512]{1,0:T(8,128)} %get-tuple-element.136), channel_id=1, source_target_pairs={{0,8},{1,9},{2,10},{3,11},{4,12},{5,13},{6,14},{7,15},{8,0},{9,1},... | collective-permute-start | bytes 18874376 | tf_op jit(solution)/shard_map/ppermute | solution.py:160
  612.9 157.0 %collective-permute-start.19 = (f32[3072,512]{1,0:T(8,128)}, f32[3072,512]{1,0:T(8,128)}, u32[]{:S(2)}, u32[]{:S(2)}) collective-permute-start(f32[3072,512]{1,0:T(8,128)} %get-tuple-element.132), channel_id=1, source_target_pairs={{0,4},{1,5},{2,6},{3,7},{4,0},{5,1},{6,2},{7,3},{8,12},{9,13},{10,... | collective-permute-start | bytes 18874376 | tf_op jit(solution)/shard_map/ppermute | solution.py:160
  664.1 116.5 %collective-permute-start.8 = (f32[1536,8,128]{2,1,0:T(8,128)}, f32[1536,8,128]{2,1,0:T(8,128)S(1)}, u32[]{:S(2)}, u32[]{:S(2)}) collective-permute-start(f32[1536,8,128]{2,1,0:T(8,128)} %get-tuple-element.93), channel_id=1, source_target_pairs={{0,1},{1,0},{2,3},{3,2},{4,5},{5,4},{6,7},{7,6},{8,9},{9,8},{10,11... | collective-permute-start | bytes 18874376 | tf_op jit(solution)/shard_map/ppermute | solution.py:160
  700.5 80.1 %collective-permute-start.16 = (f32[1536,8,128]{2,1,0:T(8,128)}, f32[1536,8,128]{2,1,0:T(8,128)}, u32[]{:S(2)}, u32[]{:S(2)}) collective-permute-start(f32[1536,8,128]{2,1,0:T(8,128)} %get-tuple-element.128), channel_id=1, source_target_pairs={{0,1},{1,0},{2,3},{3,2},{4,5},{5,4},{6,7},{7,6},{8,9},{9,8},{10,11... | collective-permute-start | bytes 18874376 | tf_op jit(solution)/shard_map/ppermute | solution.py:160
  700.6 185.9 %collective-permute-start.21 = (f32[3072,512]{1,0:T(8,128)}, f32[3072,512]{1,0:T(8,128)}, u32[]{:S(2)}, u32[]{:S(2)}) collective-permute-start(f32[3072,512]{1,0:T(8,128)} %get-tuple-element.134), channel_id=1, source_target_pairs={{0,8},{1,9},{2,10},{3,11},{4,12},{5,13},{6,14},{7,15},{8,0},{9,1},... | collective-permute-start | bytes 18874376 | tf_op jit(solution)/shard_map/ppermute | solution.py:160
  751.6 143.7 %collective-permute-start.14 = (f32[1536,8,128]{2,1,0:T(8,128)}, f32[1536,8,128]{2,1,0:T(8,128)}, u32[]{:S(2)}, u32[]{:S(2)}) collective-permute-start(f32[1536,8,128]{2,1,0:T(8,128)} %add.188), channel_id=1, source_target_pairs={{0,2},{1,3},{2,0},{3,1},{4,6},{5,7},{6,4},{7,5},{8,10},{9,11},{10,... | collective-permute-start | bytes 18874376 | tf_op jit(solution)/shard_map/ppermute | solution.py:160
  770.0 140.1 %collective-permute-start.23 = (f32[3072,512]{1,0:T(8,128)}, f32[3072,512]{1,0:T(8,128)}, u32[]{:S(2)}, u32[]{:S(2)}) collective-permute-start(f32[3072,512]{1,0:T(8,128)} %add.197), channel_id=1, source_target_pairs={{0,4},{1,5},{2,6},{3,7},{4,0},{5,1},{6,2},{7,3},{8,12},{9,13},{10,... | collective-permute-start | bytes 18874376 | tf_op jit(solution)/shard_map/ppermute | solution.py:160
  780.5 263.3 %collective-permute-start.18 = (f32[3072,512]{1,0:T(8,128)}, f32[3072,512]{1,0:T(8,128)}, u32[]{:S(2)}, u32[]{:S(2)}) collective-permute-start(f32[3072,512]{1,0:T(8,128)} %get-tuple-element.130), channel_id=1, source_target_pairs={{0,4},{1,5},{2,6},{3,7},{4,0},{5,1},{6,2},{7,3},{8,12},{9,13},{10,... | collective-permute-start | bytes 18874376 | tf_op jit(solution)/shard_map/ppermute | solution.py:160
  780.6 263.2 %collective-permute-start.20 = (f32[3072,512]{1,0:T(8,128)}, f32[3072,512]{1,0:T(8,128)}, u32[]{:S(2)}, u32[]{:S(2)}) collective-permute-start(f32[3072,512]{1,0:T(8,128)} %add.194), channel_id=1, source_target_pairs={{0,8},{1,9},{2,10},{3,11},{4,12},{5,13},{6,14},{7,15},{8,0},{9,1},... | collective-permute-start | bytes 18874376 | tf_op jit(solution)/shard_map/ppermute | solution.py:160
  886.4 175.6 %collective-permute-start.15 = (f32[1536,8,128]{2,1,0:T(8,128)}, f32[1536,8,128]{2,1,0:T(8,128)}, u32[]{:S(2)}, u32[]{:S(2)}) collective-permute-start(f32[1536,8,128]{2,1,0:T(8,128)} %get-tuple-element.125), channel_id=1, source_target_pairs={{0,1},{1,0},{2,3},{3,2},{4,5},{5,4},{6,7},{7,6},{8,9},{9,8},{10,11... | collective-permute-start | bytes 18874376 | tf_op jit(solution)/shard_map/ppermute | solution.py:160
  895.3 166.8 %collective-permute-start.17 = (f32[1536,8,128]{2,1,0:T(8,128)}, f32[1536,8,128]{2,1,0:T(8,128)}, u32[]{:S(2)}, u32[]{:S(2)}) collective-permute-start(f32[1536,8,128]{2,1,0:T(8,128)} %add.191), channel_id=1, source_target_pairs={{0,2},{1,3},{2,0},{3,1},{4,6},{5,7},{6,4},{7,5},{8,10},{9,11},{10,... | collective-permute-start | bytes 18874376 | tf_op jit(solution)/shard_map/ppermute | solution.py:160
  (21 other events, 595.4 us)

commit v2 on v1

v2 whole, which is shorter than its diff:
```python
import functools

import jax
import jax.numpy as jnp
from jax import lax
from jax.experimental import pallas as pl
from jax.experimental.pallas import tpu as pltpu
from jax.sharding import PartitionSpec as P


BF = jnp.bfloat16
F32 = jnp.float32
I32 = jnp.int32
TILE = 256
GROUP = 16
DEPTH = 4
KEY_STEP = 4096
LIST_PART = 1024
EXPERTS = ((4, 0), (8, 1), (0, 0), (0, 1), (8, 0), (4, 1), (12, 0), (12, 1))
CALLS = ((0, 0, 4), (1, 0, 2), (1, 2, 8), (0, 6, 7), (0, 7, 8), (0, 4, 6))
ANY = pl.BlockSpec(memory_space=pl.ANY)


def dot_nt(lhs, rhs):
    return lax.dot_general(lhs, rhs, (((1,), (1,)), ((), ())), preferred_element_type=F32)


def dot_tn(lhs, rhs):
    return lax.dot_general(lhs, rhs, (((0,), (0,)), ((), ())), preferred_element_type=F32)


def dot_nn(lhs, rhs):
    return jnp.dot(lhs, rhs, preferred_element_type=F32)


def tile_rows(t):
    return pl.ds(pl.multiple_of(t * TILE, TILE), TILE)


def list_stream(count, tok_hbm, gate_hbm, tok, gate, sems):
    def copies(c):
        part = pl.ds(pl.multiple_of(c * LIST_PART, LIST_PART), LIST_PART)
        return (pltpu.make_async_copy(tok_hbm.at[part], tok.at[part], sems.at[0, c]),
                pltpu.make_async_copy(gate_hbm.at[part], gate.at[part], sems.at[1, c]))

    def start(c, carry):
        for copy in copies(c):
            copy.start()
        return carry

    def wait(t):
        @pl.when(lax.rem(t, LIST_PART // TILE) == 0)
        def _():
            for copy in copies(lax.div(t, LIST_PART // TILE)):
                copy.wait()

    lax.fori_loop(0, lax.div(count * TILE + LIST_PART - 1, LIST_PART), start, 0)
    return wait


def gather_kernel(lanes, n_src, total, tok_hbm, gate_hbm, piece0, piece1, piece2, piece3, x_out, g_out, table, x_stage, g_stage, x_buf, g_buf, tok, gate, sems, out_sems, list_sems):
    count = total[0]
    half = lanes // 2
    list_wait = list_stream(count, tok_hbm, gate_hbm, tok, gate, list_sems)
    pieces = (piece0, piece1, piece2, piece3)
    copies = [pltpu.make_async_copy(ref, table.at[pl.ds(i * n_src // 2, n_src // 2)], sems.at[i]) for i, ref in enumerate(pieces)]
    for copy in copies:
        copy.start()
    table[2 * n_src] = jnp.zeros_like(table[2 * n_src])
    for copy in copies:
        copy.wait()

    def stores(t, slot):
        return (pltpu.make_async_copy(x_buf.at[slot], x_out.at[tile_rows(t)], out_sems.at[0, slot]),
                pltpu.make_async_copy(g_buf.at[slot], g_out.at[tile_rows(t)], out_sems.at[1, slot]))

    def tile(t, carry):
        slot = lax.rem(t, 2)
        base = t * TILE
        list_wait(t)

        @pl.when(t >= 2)
        def _():
            for copy in stores(t - 2, slot):
                copy.wait()

        def body(block, inner):
            row0 = block * GROUP
            for q in range(0, GROUP, 2):
                pos = base + row0 + q
                pair = [table[tok[pos + i]] for i in range(2)]
                x_pair = [both[:lanes].astype(F32) for both in pair]
                g_pair = [both[lanes:].astype(F32) * gate[pos + i] for i, both in enumerate(pair)]
                for stage, rows in ((x_stage, x_pair), (g_stage, g_pair)):
                    for h in range(2):
                        dst = pl.ds(pl.multiple_of((row0 + q) * half, lanes), lanes)
                        stage[h, dst, :] = jnp.concatenate([row[h * half:(h + 1) * half] for row in rows], axis=0)
            return inner

        lax.fori_loop(0, TILE // GROUP, body, 0)
        for c in range(lanes):
            cols = slice(c * 128, (c + 1) * 128)
            src = (c // half, pl.ds(c % half, TILE, stride=half))
            x_buf[slot, :, cols] = x_stage[src].astype(BF)
            g_buf[slot, :, cols] = g_stage[src].astype(BF)
        for copy in stores(t, slot):
            copy.start()
        return carry

    lax.fori_loop(0, count, tile, 0)
    for back in (2, 1):
        @pl.when(count >= back)
        def _():
            for copy in stores(count - back, lax.rem(count - back, 2)):
                copy.wait()


def pack_kernel(ff, gate_ref, up_ref, down_ref, a_out, b_out, buf, in_sems, out_sems):
    dim = gate_ref.shape[1]
    loads, stores = [], []
    for e, out in enumerate((a_out, b_out)):
        parts = [(gate_ref.at[e], 0, dim), (up_ref.at[e], dim, dim)]
        parts += [(down_ref.at[e, :, pl.ds(h * ff, ff)], 2 * dim + h * ff, ff) for h in range(dim // ff)]
        for i, (src, row, size) in enumerate(parts):
            rows = pl.ds(row, size)
            loads.append(pltpu.make_async_copy(src, buf.at[e, rows], in_sems.at[e, i]))
            stores.append(pltpu.make_async_copy(buf.at[e, rows], out.at[rows], out_sems.at[e, i]))
    for copy in loads:
        copy.start()
    for load, store in zip(loads, stores):
        load.wait()
        store.start()
    for copy in stores:
        copy.wait()


def expert_kernel(ff, dim, j0, n, inits, n_carried, first_tile, n_tiles, x_hbm, g_hbm, *rest):
    w_refs = rest[:n]
    given = list(rest[n:n + 3 * sum(inits)])
    init_refs = [[given.pop(0) for _ in range(3)] if has else None for has in inits]
    o_hbm, dx_hbm, *rest = rest[n + 3 * sum(inits) + n_carried:]
    p_refs = [rest[3 * i:3 * i + 3] for i in range(n)]
    w_buf, p_buf, x_buf, g_buf, o_buf, dx_buf, w_sem, i_sem, p_sem, in_sem, out_sem = rest[3 * n:]
    base = first_tile[j0]
    count = first_tile[j0 + n - 1] + n_tiles[j0 + n - 1] - base

    def loads(t, slot):
        rows = tile_rows(base + t)
        return (pltpu.make_async_copy(x_hbm.at[rows], x_buf.at[slot], in_sem.at[0, slot]),
                pltpu.make_async_copy(g_hbm.at[rows], g_buf.at[slot], in_sem.at[1, slot]))

    def stores(t, slot):
        rows = tile_rows(base + t)
        return (pltpu.make_async_copy(o_buf.at[slot], o_hbm.at[rows], out_sem.at[0, slot]),
                pltpu.make_async_copy(dx_buf.at[slot], dx_hbm.at[rows], out_sem.at[1, slot]))

    def w_copy(i):
        return pltpu.make_async_copy(w_refs[i], w_buf.at[i % 2], w_sem.at[i % 2])

    def init_copy(i):
        return [pltpu.make_async_copy(init_refs[i][c], p_buf.at[i % 3, pl.ds(c * dim, dim)], i_sem.at[i % 3, c]) for c in range(3)]

    def flush(i):
        return [pltpu.make_async_copy(p_buf.at[i % 3, pl.ds(c * dim, dim)], p_refs[i][c], p_sem.at[i % 3, c]) for c in range(3)]

    def start_all(copies):
        for copy in copies:
            copy.start()

    def wait_all(copies):
        for copy in copies:
            copy.wait()

    for copy in loads(0, 0):
        copy.start()
    for i in range(min(n, 2)):
        w_copy(i).start()
    for i in range(min(n, 2)):
        if inits[i]:
            start_all(init_copy(i))

    def tile(t, carry):
        slot = lax.rem(t, 2)
        place = base + t
        which = jnp.int32(0)
        for i in range(1, n):
            which = which + (place >= first_tile[j0 + i]).astype(I32)

        @pl.when(t + 1 < count)
        def _():
            for copy in loads(t + 1, 1 - slot):
                copy.start()

        for i in range(n):
            @pl.when(place == first_tile[j0 + i])
            def _():
                w_copy(i).wait()
                if 1 <= i < n - 1:
                    w_copy(i + 1).start()
                if i >= 2:
                    wait_all(flush(i - 2))
                if 1 <= i < n - 1 and inits[i + 1]:
                    start_all(init_copy(i + 1))
                if not inits[i]:
                    def clear(r, inner):
                        p_buf[i % 3, pl.ds(pl.multiple_of(r * 64, 64), 64), :] = jnp.zeros((64, ff), F32)
                        return inner

                    lax.fori_loop(0, 3 * dim // 64, clear, 0)

        @pl.when(t >= 2)
        def _():
            for copy in stores(t - 2, slot):
                copy.wait()

        for copy in loads(t, slot):
            copy.wait()
        w_ref = w_buf.at[lax.rem(which, 2)]
        p_ref = p_buf.at[lax.rem(which, 3)]
        x_rows = x_buf[slot]
        g_rows = g_buf[slot]
        gate_w = w_ref[0:dim, :]
        up_w = w_ref[dim:2 * dim, :]
        u_val = dot_nn(x_rows, gate_w)
        v_val = dot_nn(x_rows, up_w)
        sig = jax.nn.sigmoid(u_val)
        act = (u_val * sig * v_val).astype(BF)
        halves = dim // ff
        d_act = None
        for h in range(halves):
            down = w_ref[2 * dim + h * ff:2 * dim + (h + 1) * ff, :]
            o_buf[slot, :, h * ff:(h + 1) * ff] = dot_nn(act, down).astype(BF)
            part = dot_nt(g_rows[:, h * ff:(h + 1) * ff], down)
            d_act = part if d_act is None else d_act + part
        d_u = (d_act * v_val * sig * (1.0 + u_val * (1.0 - sig))).astype(BF)
        d_v = (d_act * u_val * sig).astype(BF)
        dx_buf[slot] = (dot_nt(d_u, gate_w) + dot_nt(d_v, up_w)).astype(BF)
        for copy in stores(t, slot):
            copy.start()
        for i in range(n):
            if inits[i]:
                @pl.when(place == first_tile[j0 + i])
                def _():
                    wait_all(init_copy(i))
        p_ref[0:dim, :] += dot_tn(x_rows, d_u)
        p_ref[dim:2 * dim, :] += dot_tn(x_rows, d_v)
        for h in range(halves):
            p_ref[2 * dim + h * ff:2 * dim + (h + 1) * ff, :] += dot_tn(act, g_rows[:, h * ff:(h + 1) * ff])

        for i in range(n):
            @pl.when(place == first_tile[j0 + i] + n_tiles[j0 + i] - 1)
            def _():
                start_all(flush(i))
        return carry

    lax.fori_loop(0, count, tile, 0)
    for back in (2, 1):
        @pl.when(count >= back)
        def _():
            for copy in stores(count - back, lax.rem(count - back, 2)):
                copy.wait()
    for i in range(max(0, n - 2), n):
        wait_all(flush(i))


def combine_kernel(lanes, n_src, use_gate, total, tok_hbm, gate_hbm, rows_hbm, mate_out, own_out, acc, stage, buf, tok, gate, sems, in_sem, list_sems):
    count = total[0]
    list_wait = list_stream(count, tok_hbm, gate_hbm, tok, gate, list_sems)

    def load(t, slot):
        return pltpu.make_async_copy(rows_hbm.at[tile_rows(t)], buf.at[slot], in_sem.at[slot])

    for ahead in range(DEPTH - 1):
        @pl.when(ahead < count)
        def _():
            load(ahead, ahead).start()

    def clear(i, carry):
        acc[pl.ds(i * 32, 32)] = jnp.zeros((32, lanes, 128), F32)
        return carry

    lax.fori_loop(0, acc.shape[0] // 32, clear, 0)

    def tile(t, carry):
        slot = lax.rem(t, DEPTH)
        base = t * TILE

        @pl.when(t + DEPTH - 1 < count)
        def _():
            load(t + DEPTH - 1, lax.rem(t + DEPTH - 1, DEPTH)).start()

        list_wait(t)
        load(t, slot).wait()
        for c in range(lanes):
            stage[pl.ds(c, TILE, stride=lanes), :] = buf[slot, :, c * 128:(c + 1) * 128].astype(F32)

        def body(block, inner):
            row0 = block * GROUP
            dests, sums = [], []
            for q in range(GROUP):
                pos = base + row0 + q
                t_row = tok[pos]
                value = stage[pl.ds(pl.multiple_of((row0 + q) * lanes, lanes), lanes), :]
                if use_gate:
                    value = value * gate[pos]
                dests.append(t_row)
                sums.append(acc[t_row] + value)
            for t_row, total_row in zip(dests, sums):
                acc[t_row] = total_row
            return inner

        lax.fori_loop(0, TILE // GROUP, body, 0)
        return carry

    lax.fori_loop(0, count, tile, 0)
    copies = [pltpu.make_async_copy(acc.at[pl.ds(i * n_src, n_src)], ref, sems.at[i]) for i, ref in enumerate((mate_out, own_out))]
    for copy in copies:
        copy.start()
    for copy in copies:
        copy.wait()


def finish_kernel(lanes, own_ref, mate_ref, x_ref, out_ref, stage):
    rows = own_ref.shape[0]
    stage[...] = (own_ref[...] + mate_ref[...] + x_ref[...]).reshape(rows * lanes, 128)
    for c in range(lanes):
        out_ref[:, c * 128:(c + 1) * 128] = stage[pl.ds(c, rows, stride=lanes), :].astype(BF)


def solution(mesh):
    n_dev = mesh.shape['ep']

    def permute(value, mask):
        return lax.ppermute(value, 'ep', [(i, i ^ mask) for i in range(n_dev)])

    def layer(x_tok, route_idx, gates, dy_tok, w_gate, w_up, w_down):
        tok_loc, top_k = route_idx.shape
        dim, ff = w_gate.shape[1], w_gate.shape[2]
        experts = w_gate.shape[0] * n_dev
        lanes = dim // 128
        n_exp = len(EXPERTS)
        slot_cap = max(2 * tok_loc * top_k // (experts - 2), tok_loc // 2)
        max_tiles = -(-2 * slot_cap // TILE)
        n_slots = n_exp * max_tiles
        list_len = n_slots * TILE
        n_half = 2 * tok_loc
        me = lax.axis_index('ep')

        routing = jnp.concatenate([route_idx.T.astype(F32), gates.T.astype(F32)], axis=0)
        rt_mate = permute(routing, 1)
        rt_xp = permute(routing, 2)
        rt_xpm = permute(rt_xp, 1)
        w_shape = jax.ShapeDtypeStruct((3 * dim, ff), BF)
        own_a, own_b = pl.pallas_call(
            functools.partial(pack_kernel, ff),
            in_specs=[ANY] * 3, out_specs=[ANY] * 2, out_shape=[w_shape, w_shape],
            scratch_shapes=[pltpu.VMEM((2, 3 * dim, ff), BF), pltpu.SemaphoreType.DMA((2, 4)), pltpu.SemaphoreType.DMA((2, 4))],
            compiler_params=pltpu.CompilerParams(vmem_limit_bytes=16 * 1024 * 1024),
            name='pack_weights',
        )(w_gate, w_up, w_down)
        wts = {(0, 0): own_a, (0, 1): own_b}
        wts[(8, 0)] = permute(wts[(0, 0)], 8)
        wts[(4, 1)] = permute(wts[(0, 1)], 4)
        wts[(4, 0)] = permute(wts[(0, 0)], 4)
        wts[(8, 1)] = permute(wts[(0, 1)], 8)
        wts[(12, 0)] = permute(wts[(8, 0)], 4)
        wts[(12, 1)] = permute(wts[(4, 1)], 8)
        cut = tok_loc // 2
        xd_own, xd_xp, xd_mate, xd_xpm = [], [], [], []
        for i in range(2):
            part = slice(i * cut, (i + 1) * cut)
            xd_own.append(jnp.concatenate([x_tok[part].reshape(cut, lanes, 128), dy_tok[part].reshape(cut, lanes, 128)], axis=1))
            xd_xp.append(permute(xd_own[i], 2))
            xd_mate.append(permute(xd_own[i], 1))
            xd_xpm.append(permute(xd_xp[i], 1))

        rt_all = jnp.stack([jnp.stack([rt_mate, routing]), jnp.stack([rt_xpm, rt_xp])])
        route = rt_all[:, :, :top_k].astype(I32)
        gate_in = rt_all[:, :, top_k:]
        place = (route // 2) ^ me
        slot = jnp.full_like(route, n_exp)
        for j, (mask, which) in enumerate(EXPERTS):
            slot = jnp.where((place == mask) & (route % 2 == which), j, slot)
        token = lax.broadcasted_iota(I32, route.shape, 1) * tok_loc + lax.broadcasted_iota(I32, route.shape, 3)
        first_key = jnp.arange(2, dtype=I32) * (16 * KEY_STEP)
        key = (slot * KEY_STEP + token + first_key[:, None, None, None]).reshape(2, -1)
        counts = jnp.sum((slot.reshape(1, 2, -1) == jnp.arange(n_exp).reshape(n_exp, 1, 1)).astype(I32), axis=2).T
        n_tiles = jnp.maximum(1, (counts + TILE - 1) // TILE)
        need = n_tiles * TILE - counts
        pad_key = jnp.where(jnp.arange(TILE) < need[:, :, None], jnp.arange(n_exp)[:, None] * KEY_STEP + n_half, n_exp * KEY_STEP) + first_key[:, None, None]
        keys = jnp.concatenate([key, pad_key.reshape(2, -1)], axis=1)
        vals = jnp.concatenate([gate_in.reshape(2, -1), jnp.zeros((2, n_exp * TILE), F32)], axis=1)
        keys, vals = lax.sort((keys.reshape(-1), vals.reshape(-1)), num_keys=1)
        per_half = n_half * top_k + n_exp * TILE
        tile_ends = jnp.cumsum(n_tiles, axis=1)
        lists = [(tile_ends[h, n_exp - 1:], keys[h * per_half:][:list_len] & (KEY_STEP - 1), vals[h * per_half:][:list_len]) for h in range(2)]
        tiles = [(tile_ends[h] - n_tiles[h], n_tiles[h]) for h in range(2)]

        row_shape = jax.ShapeDtypeStruct((list_len, dim), BF)
        tile_buf = pltpu.VMEM((2, TILE, dim), BF)
        stage_buf = pltpu.VMEM((TILE * lanes, 128), F32)
        half_buf = pltpu.VMEM((2, TILE * lanes // 2, 128), F32)
        list_bufs = (pltpu.SMEM((list_len,), I32), pltpu.SMEM((list_len,), F32))
        list_sems = pltpu.SemaphoreType.DMA((2, list_len // LIST_PART))

        def gather(lists, pieces):
            return pl.pallas_call(
                functools.partial(gather_kernel, lanes, tok_loc),
                grid_spec=pltpu.PrefetchScalarGridSpec(
                    num_scalar_prefetch=1, grid=(), in_specs=[ANY] * 6, out_specs=[ANY, ANY],
                    scratch_shapes=[pltpu.VMEM((n_half + 8, 2 * lanes, 128), BF), half_buf, half_buf, tile_buf, tile_buf, *list_bufs, pltpu.SemaphoreType.DMA((4,)), pltpu.SemaphoreType.DMA((2, 2)), list_sems]),
                out_shape=[row_shape, row_shape],
                compiler_params=pltpu.CompilerParams(vmem_limit_bytes=48 * 1024 * 1024),
                name='gather_rows',
            )(*lists, *pieces)

        def experts_call(call, tiles, rows, carried, inits):
            _, lo, hi = call
            n = hi - lo
            keys = EXPERTS[lo:hi]
            given = [part for k in keys if k in inits for part in inits[k]]
            extra = [wts[k] for k in keys] + given + list(carried)
            first_alias = 4 + n + len(given)
            grad = jax.ShapeDtypeStruct((dim, ff), F32)
            o_rows, dx_rows, *parts = pl.pallas_call(
                functools.partial(expert_kernel, ff, dim, lo, n, tuple(k in inits for k in keys), len(carried)),
                grid_spec=pltpu.PrefetchScalarGridSpec(
                    num_scalar_prefetch=2, grid=(), in_specs=[ANY] * (2 + len(extra)), out_specs=[ANY] * (2 + 3 * n),
                    scratch_shapes=[pltpu.VMEM((2, 3 * dim, ff), BF), pltpu.VMEM((3, 3 * dim, ff), F32), tile_buf, tile_buf, tile_buf, tile_buf,
                                    pltpu.SemaphoreType.DMA((2,)), pltpu.SemaphoreType.DMA((3, 3)), pltpu.SemaphoreType.DMA((3, 3)), pltpu.SemaphoreType.DMA((2, 2)), pltpu.SemaphoreType.DMA((2, 2))]),
                out_shape=[row_shape, row_shape] + [grad] * (3 * n),
                input_output_aliases={first_alias: 0, first_alias + 1: 1} if carried else {},
                compiler_params=pltpu.CompilerParams(vmem_limit_bytes=56 * 1024 * 1024),
                name='expert_steps',
            )(*tiles, *rows, *extra)
            return (o_rows, dx_rows), {k: tuple(parts[3 * i:3 * i + 3]) for i, k in enumerate(keys)}

        def combine(lists, rows, use_gate):
            block = jax.ShapeDtypeStruct((tok_loc, lanes, 128), F32)
            return pl.pallas_call(
                functools.partial(combine_kernel, lanes, tok_loc, use_gate),
                grid_spec=pltpu.PrefetchScalarGridSpec(
                    num_scalar_prefetch=1, grid=(), in_specs=[ANY] * 3, out_specs=[ANY, ANY],
                    scratch_shapes=[pltpu.VMEM((n_half + 32, lanes, 128), F32), stage_buf, pltpu.VMEM((DEPTH, TILE, dim), BF), *list_bufs, pltpu.SemaphoreType.DMA((2,)), pltpu.SemaphoreType.DMA((DEPTH,)), list_sems]),
                out_shape=[block, block],
                compiler_params=pltpu.CompilerParams(vmem_limit_bytes=48 * 1024 * 1024),
                name='combine_rows',
            )(*lists, rows)

        rows = (gather(lists[0], xd_mate + xd_own), gather(lists[1], xd_xpm + xd_xp))
        outs, grads = [(), ()], {}
        for call in CALLS:
            half = call[0]
            outs[half], parts = experts_call(call, tiles[half], rows[half], outs[half], grads)
            grads = {**grads, **parts}
        out0, out1 = outs
        lists0, lists1 = lists

        def settle_rows(which, use_gate):
            mate1, own1 = combine(lists1, out1[which], use_gate)
            mate1 = permute(mate1, 1)
            to_x = own1 + mate1
            from_x = permute(to_x, 2)
            mate0, own0 = combine(lists0, out0[which], use_gate)
            mate0 = permute(mate0, 1)
            rows_in = pl.BlockSpec((TILE, lanes, 128), lambda i: (i, 0, 0))
            return pl.pallas_call(
                functools.partial(finish_kernel, lanes), grid=(tok_loc // TILE,), in_specs=[rows_in] * 3,
                out_specs=pl.BlockSpec((TILE, dim), lambda i: (i, 0)), out_shape=jax.ShapeDtypeStruct((tok_loc, dim), BF),
                scratch_shapes=[stage_buf], compiler_params=pltpu.CompilerParams(vmem_limit_bytes=24 * 1024 * 1024), name='finish_rows',
            )(own0, mate0, from_x)

        y_tok = settle_rows(0, True)
        dx_tok = settle_rows(1, False)

        totals = []
        for c in range(3):
            def back(key, mask, value=None):
                return permute(grads[key][c] if value is None else value, mask)

            via_a = grads[(8, 0)][c] + back((12, 0), 4)
            via_b = grads[(4, 1)][c] + back((12, 1), 8)
            g_a = grads[(0, 0)][c] + back((4, 0), 4) + back((8, 0), 8, via_a)
            g_b = grads[(0, 1)][c] + back((8, 1), 8) + back((4, 1), 4, via_b)
            totals.append(jnp.stack([g_a, g_b]))
        d_down = jnp.concatenate([totals[2][:, h * ff:(h + 1) * ff] for h in range(dim // ff)], axis=2)
        return y_tok, dx_tok, totals[0], totals[1], d_down

    return jax.shard_map(layer, mesh=mesh, in_specs=(P('ep'),) * 7, out_specs=(P('ep'),) * 5, check_vma=False)
```

time: 1080 us -> 1140 us (1.056)
  waiting for transfers between devices: 360 us -> 574 us
  Pallas kernels: 490 us -> 400 us
  other arithmetic: 128 us -> 96.7 us
  local copies, waits for them, and re-layouts: 49 us -> 18.5 us
    ppermute x24 -> x39, waiting for transfers between devices: 360 us -> 574 us  [permute(): return lax.ppermute(value, 'ep', [(i, i ^ mask) for i in range(n_dev)])]
    pallas_call x16 -> x9, Pallas kernels: 267 us -> 227 us  [the longest x6 213 us: experts_call(): pl.pallas_call(functools.partial(expert_kernel, ff, dim, lo, n, tuple((k...]
    pallas_call x4, Pallas kernels: 146 us -> 116 us  [combine(): pl.pallas_call(functools.partial(combine_kernel, lanes, tok_loc, use_gate...]
    another operation x11 -> x1, local copies, waits for them, and re-layouts: 24.2 us -> 0.02 us  [the longest x4 20.4 us: plan(): counts = jnp.stack([jnp.sum((slot == j).astype(I32)) for j in range(n_exp)])]
    pallas_call x2, Pallas kernels: 77.9 us -> 57.4 us  [gather(): pl.pallas_call(functools.partial(gather_kernel, lanes, tok_loc), grid_spe...]
    concatenate x5 -> x1, other arithmetic: 15.2 us -> 2.42 us  [layer(): jnp.concatenate([totals[2][:, h * ff:(h + 1) * ff] for h in range(dim //...]
    add x6 -> x10, other arithmetic: 34 us -> 28 us  [the longest x3 11.3 us: layer(): via_b = grads[4, 1][c] + back((12, 1), 8)]
    ppermute x24 -> x39, starting transfers between devices: 44.6 us -> 40.5 us  [permute(): return lax.ppermute(value, 'ep', [(i, i ^ mask) for i in range(n_dev)])]
  transfers between devices with their start and end apart: 24 -> 39, of which waited for: 6 -> 15; matrix products, arithmetic and copies ran while one was open for 14% -> 9% of each run, Pallas kernels for 26% -> 35%
where the time goes in v2:
time: 1140 us; the launch traced here: 1130 us
  waiting for transfers between devices  574 us (50%)
  Pallas kernels  400 us (35%)
  other arithmetic  96.7 us (8%)
  starting transfers between devices  40.5 us (4%)
  local copies, waits for them, and re-layouts  18.5 us (2%)
    ppermute x39, waiting for transfers between devices, permute(): return lax.ppermute(value, 'ep', [(i, i ^ mask) for i in range(n_dev)])  574 us
    pallas_call x6, Pallas kernels, experts_call(): pl.pallas_call(functools.partial(expert_kernel, ff, dim, lo, n, tuple((k...  213 us
    pallas_call x4, Pallas kernels, combine(): pl.pallas_call(functools.partial(combine_kernel, lanes, tok_loc, use_gate...  116 us
    pallas_call x2, Pallas kernels, gather(): pl.pallas_call(functools.partial(gather_kernel, lanes, tok_loc), grid_spe...  57.4 us
    ppermute x39, starting transfers between devices, permute(): return lax.ppermute(value, 'ep', [(i, i ^ mask) for i in range(n_dev)])  40.5 us
    sort x1, other arithmetic, layer(): keys, vals = lax.sort((keys.reshape(-1), vals.reshape(-1)), num_keys=1)  39 us
    another operation x9, other arithmetic, layer(): totals.append(jnp.stack([g_a, g_b]))  23.1 us
  transfers between devices with their start and end apart: 39, of which 15 were waited for; matrix products, arithmetic and copies ran while one was open for 9% of the time, Pallas kernels for 35%

profile of v2, /device:TPU:0, one launch (start us, length us, event | category | flops | bytes accessed | tf_op | source)
XLA Modules:
  0.0 1131.8 jit_solution(4251013682167369270)
XLA Ops:
  14.6 67.6 %collective-permute-done.1 = f32[16,1536]{1,0:T(8,128)S(1)} collective-permute-done((f32[16,1536]{1,0:T(8,128)S(1)}, f32[16,1536]{1,0:T(8,128)S(1)}, u32[]{:S(2)}, u32[]{:S(2)}) %collective-permute-start.1) | collective-permute-done | bytes 98336 | tf_op jit(solution)/shard_map/ppermute | solution.py:334
  93.2 61.1 %collective-permute-done.9.piece3 = bf16[768,16,128]{2,1,0:T(8,128)(2,1)} collective-permute-done((bf16[768,16,128]{2,1,0:T(8,128)(2,1)}, bf16[768,16,128]{2,1,0:T(8,128)(2,1)}, u32[]{:S(2)}, u32[]{:S(2)}) %collective-permute-start.9) | collective-permute-done | bytes 3145760 | tf_op jit(solution)/shard_map/ppermute | solution.py:334
  167.7 59.0 %collective-permute-done.6.rest_3_.rest_1_ = bf16[3072,512]{1,0:T(8,128)(2,1)} collective-permute-done((bf16[3072,512]{1,0:T(8,128)(2,1)}, bf16[3072,512]{1,0:T(8,128)(2,1)}, u32[]{:S(2)}, u32[]{:S(2)}) %collective-permute-start.6) | collective-permute-done | bytes 3145760 | tf_op jit(solution)/shard_map/ppermute | solution.py:334
  228.4 39.0 %sort.23 = (s32[53248]{0:T(1024)S(1)}, f32[53248]{0:T(1024)S(1)}, s32[53248]{0:T(1024)}) sort(s32[53248]{0:T(1024)S(1)} %bitcast.95, f32[53248]{0:T(1024)S(1)} %bitcast.96, s32[53248]{0:T(1024)S(1)} %iota.41), dimensions={0}, to_apply=%region_2.3 | sort | flops 851968 | bytes 1277952 | tf_op jit(solution)/shard_map/sort | solution.py:393
  268.1 28.3 %gather_rows.2 = (bf16[14336,1024]{1,0:T(8,128)(2,1)}, bf16[14336,1024]{1,0:T(8,128)(2,1)}) custom-call(s32[1]{0:T(128)} %bitcast.9.total, s32[14336]{0:T(1024)S(1)} %get-tuple-element.170.tok_hbm, f32[14336]{0:T(1024)S(1)} %get-tuple-element.168.gate_hbm, bf16[768,16,128]{2,1,0:T(8,128)(2,1)} %collective-permute-done.3.piece0, ...), custom_call_target="tpu_custom_call" | custom-call | tf_op jit(solution)/shard_map/gather_rows/pallas_call | solution.py:407
  296.4 48.6 %expert_steps.6 = (bf16[14336,1024]{1,0:T(8,128)(2,1)}, bf16[14336,1024]{1,0:T(8,128)(2,1)}, f32[1024,512]{1,0:T(8,128)}, f32[1024,512]{1,0:T(8,128)}, f32[1024,...) custom-call(s32[8]{0:T(128)} %get-tuple-element.174.first_tile, ...), custom_call_target="tpu_custom_call" | custom-call | tf_op jit(solution)/shard_map/expert_steps/pallas_call | solution.py:425
  345.0 29.1 %gather_rows.3 = (bf16[14336,1024]{1,0:T(8,128)(2,1)}, bf16[14336,1024]{1,0:T(8,128)(2,1)}) custom-call(s32[1]{0:T(128)} %bitcast.14.total, s32[14336]{0:T(1024)S(1)} %get-tuple-element.169.tok_hbm, f32[14336]{0:T(1024)S(1)} %get-tuple-element.167.gate_hbm, bf16[768,16,128]{2,1,0:T(8,128)(2,1)} %collective-permute-done.8.piece0, ...), custom_call_target="tpu_custom_call" | custom-call | tf_op jit(solution)/shard_map/gather_rows/pallas_call | solution.py:407
  374.2 28.2 %expert_steps.7 = (bf16[14336,1024]{1,0:T(8,128)(2,1)}, bf16[14336,1024]{1,0:T(8,128)(2,1)}, f32[1024,512]{1,0:T(8,128)}, f32[1024,512]{1,0:T(8,128)}, f32[1024,...) custom-call(s32[8]{0:T(128)} %get-tuple-element.173.first_tile, ...), custom_call_target="tpu_custom_call" | custom-call | tf_op jit(solution)/shard_map/expert_steps/pallas_call | solution.py:425
  409.8 76.8 %expert_steps.8 = (bf16[14336,1024]{1,0:T(8,128)(2,1)}, bf16[14336,1024]{1,0:T(8,128)(2,1)}, f32[1024,512]{1,0:T(8,128)}, f32[1024,512]{1,0:T(8,128)}, f32[1024,...) custom-call(s32[8]{0:T(128)} %get-tuple-element.173.first_tile, ...), custom_call_target="tpu_custom_call", output_to_operand_aliasing={{0}: (16, {}), {1}: (17, {})} | custom-call | tf_op jit(solution)/shard_map/expert_steps/pallas_call | solution.py:425
  486.6 31.8 %combine_rows.5 = (f32[1536,8,128]{2,1,0:T(8,128)}, f32[1536,8,128]{2,1,0:T(8,128)}) custom-call(s32[1]{0:T(128)} %bitcast.14.total, s32[14336]{0:T(1024)S(1)} %get-tuple-element.169.tok_hbm, f32[14336]{0:T(1024)S(1)} %get-tuple-element.167.gate_hbm, bf16[14336,1024]{1,0:T(8,128)(2,1)} %get-tuple-element.126.rows_hbm), custom_call_target="tpu_custom_call" | custom-call | tf_op jit(solution)/shard_map/combine_rows/pallas_call | solution.py:440
  519.7 26.5 %combine_rows.7 = (f32[1536,8,128]{2,1,0:T(8,128)}, f32[1536,8,128]{2,1,0:T(8,128)}) custom-call(s32[1]{0:T(128)} %bitcast.14.total, s32[14336]{0:T(1024)S(1)} %get-tuple-element.169.tok_hbm, f32[14336]{0:T(1024)S(1)} %get-tuple-element.167.gate_hbm, bf16[14336,1024]{1,0:T(8,128)(2,1)} %get-tuple-element.132.rows_hbm), custom_call_target="tpu_custom_call" | custom-call | tf_op jit(solution)/shard_map/combine_rows/pallas_call | solution.py:440
  546.3 16.3 %expert_steps.9 = (bf16[14336,1024]{1,0:T(8,128)(2,1)}, bf16[14336,1024]{1,0:T(8,128)(2,1)}, f32[1024,512]{1,0:T(8,128)}, f32[1024,512]{1,0:T(8,128)}, f32[1024,512]{1,0:T(8,128)}) custom-call(s32[8]{0:T(128)} %get-tuple-element.174.first_tile, s32[8]{0:T(128)} %get-tuple-element.178.n_tiles, ...), custom_call_target="tpu_custom_call", output_to_operand_aliasing={{0}: (8, {}), {1}: (9, {})} | custom-call | tf_op jit(solution)/shard_map/expert_steps/pallas_call | solution.py:425
  562.6 16.2 %expert_steps.10 = (bf16[14336,1024]{1,0:T(8,128)(2,1)}, bf16[14336,1024]{1,0:T(8,128)(2,1)}, f32[1024,512]{1,0:T(8,128)}, f32[1024,512]{1,0:T(8,128)}, f32[1024,512]{1,0:T(8,128)}) custom-call(s32[8]{0:T(128)} %get-tuple-element.174.first_tile, s32[8]{0:T(128)} %get-tuple-element.178.n_tiles, ...), custom_call_target="tpu_custom_call", output_to_operand_aliasing={{0}: (8, {}), {1}: (9, {})} | custom-call | tf_op jit(solution)/shard_map/expert_steps/pallas_call | solution.py:425
  581.0 46.7 %collective-permute-done.36 = f32[1024,512]{1,0:T(8,128)} collective-permute-done((f32[1024,512]{1,0:T(8,128)}, f32[1024,512]{1,0:T(8,128)}, u32[]{:S(2)}, u32[]{:S(2)}) %collective-permute-start.36) | collective-permute-done | bytes 2097184 | tf_op jit(solution)/shard_map/ppermute | solution.py:334
  627.7 44.9 %collective-permute-done.25 = f32[1024,512]{1,0:T(8,128)} collective-permute-done((f32[1024,512]{1,0:T(8,128)}, f32[1024,512]{1,0:T(8,128)}, u32[]{:S(2)}, u32[]{:S(2)}) %collective-permute-start.25) | collective-permute-done | bytes 2097184 | tf_op jit(solution)/shard_map/ppermute | solution.py:334
  678.1 39.5 %collective-permute-done.31 = f32[1024,512]{1,0:T(8,128)} collective-permute-done((f32[1024,512]{1,0:T(8,128)}, f32[1024,512]{1,0:T(8,128)}, u32[]{:S(2)}, u32[]{:S(2)}) %collective-permute-start.31) | collective-permute-done | bytes 2097184 | tf_op jit(solution)/shard_map/ppermute | solution.py:334
  723.0 27.3 %expert_steps.11 = (bf16[14336,1024]{1,0:T(8,128)(2,1)}, bf16[14336,1024]{1,0:T(8,128)(2,1)}, f32[1024,512]{1,0:T(8,128)}, f32[1024,512]{1,0:T(8,128)}, f32[1024...) custom-call(s32[8]{0:T(128)} %get-tuple-element.174.first_tile, ...), custom_call_target="tpu_custom_call", output_to_operand_aliasing={{0}: (12, {}), {1}: (13, {})} | custom-call | tf_op jit(solution)/shard_map/expert_steps/pallas_call | solution.py:425
  774.1 31.3 %combine_rows.4 = (f32[1536,8,128]{2,1,0:T(8,128)}, f32[1536,8,128]{2,1,0:T(8,128)}) custom-call(s32[1]{0:T(128)} %bitcast.9.total, s32[14336]{0:T(1024)S(1)} %copy-done.6, f32[14336]{0:T(1024)S(1)} %copy-done.8, bf16[14336,1024]{1,0:T(8,128)(2,1)} %get-tuple-element.123.rows_hbm), custom_call_target="tpu_custom_call" | custom-call | tf_op jit(solution)/shard_map/combine_rows/pallas_call | solution.py:440
  805.5 26.3 %combine_rows.6 = (f32[1536,8,128]{2,1,0:T(8,128)}, f32[1536,8,128]{2,1,0:T(8,128)}) custom-call(s32[1]{0:T(128)} %bitcast.9.total, s32[14336]{0:T(1024)S(1)} %copy-done.6, f32[14336]{0:T(1024)S(1)} %copy-done.8, bf16[14336,1024]{1,0:T(8,128)(2,1)} %get-tuple-element.129.rows_hbm), custom_call_target="tpu_custom_call" | custom-call | tf_op jit(solution)/shard_map/combine_rows/pallas_call | solution.py:440
  855.8 44.9 %collective-permute-done.32 = f32[1024,512]{1,0:T(8,128)} collective-permute-done((f32[1024,512]{1,0:T(8,128)}, f32[1024,512]{1,0:T(8,128)}, u32[]{:S(2)}, u32[]{:S(2)}) %collective-permute-start.32) | collective-permute-done | bytes 2097184 | tf_op jit(solution)/shard_map/ppermute | solution.py:334
  900.7 43.6 %collective-permute-done.38 = f32[1024,512]{1,0:T(8,128)} collective-permute-done((f32[1024,512]{1,0:T(8,128)}, f32[1024,512]{1,0:T(8,128)}, u32[]{:S(2)}, u32[]{:S(2)}) %collective-permute-start.38) | collective-permute-done | bytes 2097184 | tf_op jit(solution)/shard_map/ppermute | solution.py:334
  953.0 40.0 %collective-permute-done.35 = f32[1024,512]{1,0:T(8,128)S(1)} collective-permute-done((f32[1024,512]{1,0:T(8,128)S(1)}, f32[1024,512]{1,0:T(8,128)S(1)}, u32[]{:S(2)}, u32[]{:S(2)}) %collective-permute-start.35) | collective-permute-done | bytes 2097184 | tf_op jit(solution)/shard_map/ppermute | solution.py:334
  1010.1 29.1 %collective-permute-done.29 = f32[1024,512]{1,0:T(8,128)} collective-permute-done((f32[1024,512]{1,0:T(8,128)S(1)}, f32[1024,512]{1,0:T(8,128)}, u32[]{:S(2)}, u32[]{:S(2)}) %collective-permute-start.29) | collective-permute-done | bytes 2097184 | tf_op jit(solution)/shard_map/ppermute | solution.py:334
  1049.2 74.1 %collective-permute-done.20.x_ref = f32[1536,8,128]{2,1,0:T(8,128)} collective-permute-done((f32[1536,8,128]{2,1,0:T(8,128)S(1)}, f32[1536,8,128]{2,1,0:T(8,128)}, u32[]{:S(2)}, u32[]{:S(2)}) %collective-permute-start.20) | collective-permute-done | bytes 6291488 | tf_op jit(solution)/shard_map/ppermute | solution.py:334
  (199 shorter events, 154.0 us)
Async XLA Ops:
  91.3 135.4 %collective-permute-start.6 = (bf16[3072,512]{1,0:T(8,128)(2,1)}, bf16[3072,512]{1,0:T(8,128)(2,1)}, u32[]{:S(2)}, u32[]{:S(2)}) collective-permute-start(bf16[3072,512]{1,0:T(8,128)(2,1)} %copy-done.1), channel_id=1, source_target_pairs={{0,4},{1,5},{2,6},{3,7},{4,0},{5,1},{6,2},{7,3},{8,12},{9,13},{10,... | collective-permute-start | bytes 9437192 | tf_op jit(solution)/shard_map/ppermute | solution.py:334
  154.2 142.2 %collective-permute-start.14 = (bf16[3072,512]{1,0:T(8,128)(2,1)}, bf16[3072,512]{1,0:T(8,128)(2,1)}, u32[]{:S(2)}, u32[]{:S(2)}) collective-permute-start(bf16[3072,512]{1,0:T(8,128)(2,1)} %copy-done.1), channel_id=1, source_target_pairs={{0,8},{1,9},{2,10},{3,11},{4,12},{5,13},{6,14},{7,15},{8,0},{9,1},... | collective-permute-start | bytes 9437192 | tf_op jit(solution)/shard_map/ppermute | solution.py:334
  156.1 189.0 %collective-permute-start.8 = (bf16[768,16,128]{2,1,0:T(8,128)(2,1)}, bf16[768,16,128]{2,1,0:T(8,128)(2,1)}, u32[]{:S(2)}, u32[]{:S(2)}) collective-permute-start(bf16[768,16,128]{2,1,0:T(8,128)(2,1)} %collective-permute-done.7.piece2), channel_id=1, source_target_pairs={{0,1},{1,0},{2,3},{3,2},{4,5},{5,4},{6,7},{7,6},{8,9},{9,8},{10,11... | collective-permute-start | bytes 9437192 | tf_op jit(solution)/shard_map/ppermute | solution.py:334
  159.3 185.8 %collective-permute-start.10 = (bf16[768,16,128]{2,1,0:T(8,128)(2,1)}, bf16[768,16,128]{2,1,0:T(8,128)(2,1)}, u32[]{:S(2)}, u32[]{:S(2)}) collective-permute-start(bf16[768,16,128]{2,1,0:T(8,128)(2,1)} %collective-permute-done.9.piece3), channel_id=1, source_target_pairs={{0,1},{1,0},{2,3},{3,2},{4,5},{5,4},{6,7},{7,6},{8,9},{9,8},{10,11... | collective-permute-start | bytes 9437192 | tf_op jit(solution)/shard_map/ppermute | solution.py:334
  166.2 240.9 %collective-permute-start.11 = (bf16[3072,512]{1,0:T(8,128)(2,1)}, bf16[3072,512]{1,0:T(8,128)(2,1)}, u32[]{:S(2)}, u32[]{:S(2)}) collective-permute-start(bf16[3072,512]{1,0:T(8,128)(2,1)} %collective-permute-done.5.rest_2_.rest_0_), channel_id=1, source_target_pairs={{0,4},{1,5},{2,6},{3,7},{4,0},{5,1},{6,2},{7,3},{8,12},{9,13},{10,... | collective-permute-start | bytes 9437192 | tf_op jit(solution)/shard_map/ppermute | solution.py:334
  226.7 181.1 %collective-permute-start.12 = (bf16[3072,512]{1,0:T(8,128)(2,1)}, bf16[3072,512]{1,0:T(8,128)(2,1)}, u32[]{:S(2)}, u32[]{:S(2)}) collective-permute-start(bf16[3072,512]{1,0:T(8,128)(2,1)} %collective-permute-done.6.rest_3_.rest_1_), channel_id=1, source_target_pairs={{0,8},{1,9},{2,10},{3,11},{4,12},{5,13},{6,14},{7,15},{8,0},{9,1},... | collective-permute-start | bytes 9437192 | tf_op jit(solution)/shard_map/ppermute | solution.py:334
  402.4 116.0 %collective-permute-start.21 = (f32[1024,512]{1,0:T(8,128)}, f32[1024,512]{1,0:T(8,128)S(1)}, u32[]{:S(2)}, u32[]{:S(2)}) collective-permute-start(f32[1024,512]{1,0:T(8,128)} %get-tuple-element.136), channel_id=1, source_target_pairs={{0,4},{1,5},{2,6},{3,7},{4,0},{5,1},{6,2},{7,3},{8,12},{9,13},{10,... | collective-permute-start | bytes 6291464 | tf_op jit(solution)/shard_map/ppermute | solution.py:334
  405.7 140.5 %collective-permute-start.24 = (f32[1024,512]{1,0:T(8,128)}, f32[1024,512]{1,0:T(8,128)}, u32[]{:S(2)}, u32[]{:S(2)}) collective-permute-start(f32[1024,512]{1,0:T(8,128)} %get-tuple-element.140), channel_id=1, source_target_pairs={{0,8},{1,9},{2,10},{3,11},{4,12},{5,13},{6,14},{7,15},{8,0},{9,1},... | collective-permute-start | bytes 6291464 | tf_op jit(solution)/shard_map/ppermute | solution.py:334
  407.0 171.8 %collective-permute-start.27 = (f32[1024,512]{1,0:T(8,128)}, f32[1024,512]{1,0:T(8,128)}, u32[]{:S(2)}, u32[]{:S(2)}) collective-permute-start(f32[1024,512]{1,0:T(8,128)} %get-tuple-element.144), channel_id=1, source_target_pairs={{0,4},{1,5},{2,6},{3,7},{4,0},{5,1},{6,2},{7,3},{8,12},{9,13},{10,... | collective-permute-start | bytes 6291464 | tf_op jit(solution)/shard_map/ppermute | solution.py:334
  407.0 171.8 %collective-permute-start.30 = (f32[1024,512]{1,0:T(8,128)}, f32[1024,512]{1,0:T(8,128)}, u32[]{:S(2)}, u32[]{:S(2)}) collective-permute-start(f32[1024,512]{1,0:T(8,128)} %get-tuple-element.148), channel_id=1, source_target_pairs={{0,8},{1,9},{2,10},{3,11},{4,12},{5,13},{6,14},{7,15},{8,0},{9,1},... | collective-permute-start | bytes 6291464 | tf_op jit(solution)/shard_map/ppermute | solution.py:334
  407.8 173.1 %collective-permute-start.33 = (f32[1024,512]{1,0:T(8,128)}, f32[1024,512]{1,0:T(8,128)}, u32[]{:S(2)}, u32[]{:S(2)}) collective-permute-start(f32[1024,512]{1,0:T(8,128)} %get-tuple-element.152), channel_id=1, source_target_pairs={{0,4},{1,5},{2,6},{3,7},{4,0},{5,1},{6,2},{7,3},{8,12},{9,13},{10,... | collective-permute-start | bytes 6291464 | tf_op jit(solution)/shard_map/ppermute | solution.py:334
  519.7 248.7 %collective-permute-start.16 = (f32[1536,8,128]{2,1,0:T(8,128)}, f32[1536,8,128]{2,1,0:T(8,128)S(1)}, u32[]{:S(2)}, u32[]{:S(2)}) collective-permute-start(f32[1536,8,128]{2,1,0:T(8,128)} %get-tuple-element.128), channel_id=1, source_target_pairs={{0,1},{1,0},{2,3},{3,2},{4,5},{5,4},{6,7},{7,6},{8,9},{9,8},{10,11... | collective-permute-start | bytes 18874376 | tf_op jit(solution)/shard_map/ppermute | solution.py:334
  546.2 227.3 %collective-permute-start.19 = (f32[1536,8,128]{2,1,0:T(8,128)}, f32[1536,8,128]{2,1,0:T(8,128)}, u32[]{:S(2)}, u32[]{:S(2)}) collective-permute-start(f32[1536,8,128]{2,1,0:T(8,128)} %get-tuple-element.134), channel_id=1, source_target_pairs={{0,1},{1,0},{2,3},{3,2},{4,5},{5,4},{6,7},{7,6},{8,9},{9,8},{10,11... | collective-permute-start | bytes 18874376 | tf_op jit(solution)/shard_map/ppermute | solution.py:334
  578.9 93.7 %collective-permute-start.25 = (f32[1024,512]{1,0:T(8,128)}, f32[1024,512]{1,0:T(8,128)}, u32[]{:S(2)}, u32[]{:S(2)}) collective-permute-start(f32[1024,512]{1,0:T(8,128)} %get-tuple-element.142), channel_id=1, source_target_pairs={{0,8},{1,9},{2,10},{3,11},{4,12},{5,13},{6,14},{7,15},{8,0},{9,1},... | collective-permute-start | bytes 6291464 | tf_op jit(solution)/shard_map/ppermute | solution.py:334
  580.9 136.7 %collective-permute-start.31 = (f32[1024,512]{1,0:T(8,128)}, f32[1024,512]{1,0:T(8,128)}, u32[]{:S(2)}, u32[]{:S(2)}) collective-permute-start(f32[1024,512]{1,0:T(8,128)} %get-tuple-element.150), channel_id=1, source_target_pairs={{0,8},{1,9},{2,10},{3,11},{4,12},{5,13},{6,14},{7,15},{8,0},{9,1},... | collective-permute-start | bytes 6291464 | tf_op jit(solution)/shard_map/ppermute | solution.py:334
  627.7 134.3 %collective-permute-start.37 = (f32[1024,512]{1,0:T(8,128)}, f32[1024,512]{1,0:T(8,128)}, u32[]{:S(2)}, u32[]{:S(2)}) collective-permute-start(f32[1024,512]{1,0:T(8,128)} %get-tuple-element.158), channel_id=1, source_target_pairs={{0,8},{1,9},{2,10},{3,11},{4,12},{5,13},{6,14},{7,15},{8,0},{9,1},... | collective-permute-start | bytes 6291464 | tf_op jit(solution)/shard_map/ppermute | solution.py:334
  762.0 93.8 %collective-permute-start.26 = (f32[1024,512]{1,0:T(8,128)}, f32[1024,512]{1,0:T(8,128)}, u32[]{:S(2)}, u32[]{:S(2)}) collective-permute-start(f32[1024,512]{1,0:T(8,128)} %add.131), channel_id=1, source_target_pairs={{0,4},{1,5},{2,6},{3,7},{4,0},{5,1},{6,2},{7,3},{8,12},{9,13},{10,... | collective-permute-start | bytes 6291464 | tf_op jit(solution)/shard_map/ppermute | solution.py:334
  764.6 136.2 %collective-permute-start.32 = (f32[1024,512]{1,0:T(8,128)}, f32[1024,512]{1,0:T(8,128)}, u32[]{:S(2)}, u32[]{:S(2)}) collective-permute-start(f32[1024,512]{1,0:T(8,128)} %add.137), channel_id=1, source_target_pairs={{0,4},{1,5},{2,6},{3,7},{4,0},{5,1},{6,2},{7,3},{8,12},{9,13},{10,... | collective-permute-start | bytes 6291464 | tf_op jit(solution)/shard_map/ppermute | solution.py:334
  768.4 175.9 %collective-permute-start.38 = (f32[1024,512]{1,0:T(8,128)}, f32[1024,512]{1,0:T(8,128)}, u32[]{:S(2)}, u32[]{:S(2)}) collective-permute-start(f32[1024,512]{1,0:T(8,128)} %add.143), channel_id=1, source_target_pairs={{0,4},{1,5},{2,6},{3,7},{4,0},{5,1},{6,2},{7,3},{8,12},{9,13},{10,... | collective-permute-start | bytes 6291464 | tf_op jit(solution)/shard_map/ppermute | solution.py:334
  773.5 174.1 %collective-permute-start.23 = (f32[1024,512]{1,0:T(8,128)}, f32[1024,512]{1,0:T(8,128)}, u32[]{:S(2)}, u32[]{:S(2)}) collective-permute-start(f32[1024,512]{1,0:T(8,128)} %add.128), channel_id=1, source_target_pairs={{0,8},{1,9},{2,10},{3,11},{4,12},{5,13},{6,14},{7,15},{8,0},{9,1},... | collective-permute-start | bytes 6291464 | tf_op jit(solution)/shard_map/ppermute | solution.py:334
  839.9 205.0 %collective-permute-start.15 = (f32[1536,8,128]{2,1,0:T(8,128)}, f32[1536,8,128]{2,1,0:T(8,128)S(1)}, u32[]{:S(2)}, u32[]{:S(2)}) collective-permute-start(f32[1536,8,128]{2,1,0:T(8,128)} %get-tuple-element.125), channel_id=1, source_target_pairs={{0,1},{1,0},{2,3},{3,2},{4,5},{5,4},{6,7},{7,6},{8,9},{9,8},{10,11... | collective-permute-start | bytes 18874376 | tf_op jit(solution)/shard_map/ppermute | solution.py:334
  855.8 189.1 %collective-permute-start.17 = (f32[1536,8,128]{2,1,0:T(8,128)S(1)}, f32[1536,8,128]{2,1,0:T(8,128)S(1)}, u32[]{:S(2)}, u32[]{:S(2)}) collective-permute-start(f32[1536,8,128]{2,1,0:T(8,128)S(1)} %copy-done.9), channel_id=1, source_target_pairs={{0,2},{1,3},{2,0},{3,1},{4,6},{5,7},{6,4},{7,5},{8,10},{9,11},{10,... | collective-permute-start | bytes 18874376 | tf_op jit(solution)/shard_map/ppermute | solution.py:334
  900.7 148.5 %collective-permute-start.18 = (f32[1536,8,128]{2,1,0:T(8,128)}, f32[1536,8,128]{2,1,0:T(8,128)}, u32[]{:S(2)}, u32[]{:S(2)}) collective-permute-start(f32[1536,8,128]{2,1,0:T(8,128)} %get-tuple-element.131), channel_id=1, source_target_pairs={{0,1},{1,0},{2,3},{3,2},{4,5},{5,4},{6,7},{7,6},{8,9},{9,8},{10,11... | collective-permute-start | bytes 18874376 | tf_op jit(solution)/shard_map/ppermute | solution.py:334
  944.3 179.0 %collective-permute-start.20 = (f32[1536,8,128]{2,1,0:T(8,128)S(1)}, f32[1536,8,128]{2,1,0:T(8,128)}, u32[]{:S(2)}, u32[]{:S(2)}) collective-permute-start(f32[1536,8,128]{2,1,0:T(8,128)S(1)} %add.126), channel_id=1, source_target_pairs={{0,2},{1,3},{2,0},{3,1},{4,6},{5,7},{6,4},{7,5},{8,10},{9,11},{10,... | collective-permute-start | bytes 18874376 | tf_op jit(solution)/shard_map/ppermute | solution.py:334
  (48 other events, 2047.0 us)

commit v3 on v2

v3 whole, which is shorter than its diff:
```python
import functools

import jax
import jax.numpy as jnp
from jax import lax
from jax.experimental import pallas as pl
from jax.experimental.pallas import tpu as pltpu
from jax.sharding import PartitionSpec as P


BF = jnp.bfloat16
F32 = jnp.float32
I32 = jnp.int32
TILE = 256
GROUP = 16
DEPTH = 4
KEY_STEP = 4096
LIST_PART = 1024
GRANT = 62 * 1024 * 1024
EXPERTS = ((4, 0), (8, 1), (0, 0), (0, 1), (8, 0), (4, 1), (12, 0), (12, 1))
CALLS = ((0, 0, 4), (1, 0, 2), (1, 2, 6), (1, 6, 8), (0, 6, 8), (0, 4, 6))
DEFERRED = 2
HBM = pl.BlockSpec(memory_space=pltpu.HBM)
DMA = pltpu.SemaphoreType.DMA


def dot_nt(lhs, rhs):
    return lax.dot_general(lhs, rhs, (((1,), (1,)), ((), ())), preferred_element_type=F32)


def dot_tn(lhs, rhs):
    return lax.dot_general(lhs, rhs, (((0,), (0,)), ((), ())), preferred_element_type=F32)


def dot_nn(lhs, rhs):
    return jnp.dot(lhs, rhs, preferred_element_type=F32)


def start_all(copies):
    for copy in copies:
        copy.start()


def wait_all(copies):
    for copy in copies:
        copy.wait()


def tile_rows(t):
    return pl.ds(pl.multiple_of(t * TILE, TILE), TILE)


def pack_kernel(ff, gate_ref, up_ref, down_ref, a_out, b_out, w_buf, w_in, w_out):
    dim = gate_ref.shape[1]
    loads, stores = [], []
    for e, out in enumerate((a_out, b_out)):
        parts = [(gate_ref.at[e], 0, dim), (up_ref.at[e], dim, dim)]
        parts += [(down_ref.at[e, :, pl.ds(h * ff, ff)], 2 * dim + h * ff, ff) for h in range(dim // ff)]
        for i, (src, row, size) in enumerate(parts):
            place = pl.ds(row, size)
            loads.append(pltpu.make_async_copy(src, w_buf.at[e, place], w_in.at[e, i]))
            stores.append(pltpu.make_async_copy(w_buf.at[e, place], out.at[place], w_out.at[e, i]))
    start_all(loads)
    for load, store in zip(loads, stores):
        load.wait()
        store.start()
    wait_all(stores)


def prep_kernel(x_ref, dy_ref, xd0_out, xd1_out, rows, xd, stage, in_sems, out_sems):
    tok_loc, dim = x_ref.shape
    lanes = dim // 128
    blocks = tok_loc // TILE
    loads = [[pltpu.make_async_copy(ref.at[tile_rows(b)], rows.at[i, tile_rows(b)], in_sems.at[i, b]) for i, ref in enumerate((x_ref, dy_ref))] for b in range(blocks)]
    for pair in loads:
        start_all(pair)
    stores = []
    for b in range(blocks):
        wait_all(loads[b])
        for i in range(2):
            for c in range(lanes):
                stage[i, pl.ds(c, TILE, stride=lanes), :] = rows[i, tile_rows(b), c * 128:(c + 1) * 128].astype(F32)
            xd[tile_rows(b), i * lanes:(i + 1) * lanes, :] = stage[i].reshape(TILE, lanes, 128).astype(BF)
        out, first = (xd0_out, 0) if b < blocks // 2 else (xd1_out, blocks // 2)
        stores.append(pltpu.make_async_copy(xd.at[tile_rows(b)], out.at[tile_rows(b - first)], out_sems.at[b]))
        stores[-1].start()
    wait_all(stores)


def list_stream(first, count, tok_hbm, gate_hbm, tok, gate, sems):
    per_part = LIST_PART // TILE

    def copies(c):
        part = pl.ds(pl.multiple_of(c * LIST_PART, LIST_PART), LIST_PART)
        return (pltpu.make_async_copy(tok_hbm.at[part], tok.at[part], sems.at[0, c]),
                pltpu.make_async_copy(gate_hbm.at[part], gate.at[part], sems.at[1, c]))

    def start(c, carry):
        start_all(copies(c))
        return carry

    def wait(t):
        @pl.when((t == first) | (lax.rem(t, per_part) == 0))
        def _():
            wait_all(copies(lax.div(t, per_part)))

    lax.fori_loop(lax.div(first, per_part), lax.div(first + count + per_part - 1, per_part), start, 0)
    return wait


def table_copies(pieces, table, sems):
    size, _ = pieces[0].shape
    return [pltpu.make_async_copy(ref, table.at[pl.ds(i * size, size)], sems.at[i]) for i, ref in enumerate(pieces)]


def gather_tile(lanes, t, table, tok, gate, x_stage, g_stage, x_dst, g_dst):
    half = lanes // 2

    def body(block, carry):
        row0 = block * GROUP
        for q in range(0, GROUP, 2):
            pos = t * TILE + row0 + q
            pair = [table[pl.ds(pl.multiple_of(tok[pos + i], 2 * lanes), 2 * lanes), :] for i in range(2)]
            x_pair = [both[:lanes].astype(F32) for both in pair]
            g_pair = [both[lanes:].astype(F32) * gate[pos + i] for i, both in enumerate(pair)]
            for stage, rows in ((x_stage, x_pair), (g_stage, g_pair)):
                for h in range(2):
                    dst = pl.ds(pl.multiple_of((row0 + q) * half, lanes), lanes)
                    stage[h, dst, :] = jnp.concatenate([row[h * half:(h + 1) * half] for row in rows], axis=0)
        return carry

    lax.fori_loop(0, TILE // GROUP, body, 0)
    for c in range(lanes):
        cols = slice(c * 128, (c + 1) * 128)
        src = (c // half, pl.ds(c % half, TILE, stride=half))
        x_dst[:, cols] = x_stage[src].astype(BF)
        g_dst[:, cols] = g_stage[src].astype(BF)


def gather_kernel(lanes, total, tok_hbm, gate_hbm, *rest):
    pieces = rest[:4]
    x_out, g_out, table, x_stage, g_stage, x_buf, g_buf, tok, gate, sems, out_sems, list_sems = rest[4:]
    count = total[0]
    list_wait = list_stream(0, count, tok_hbm, gate_hbm, tok, gate, list_sems)
    copies = table_copies(pieces, table, sems)
    start_all(copies)
    pad_rows = pl.ds(table.shape[0] - 16 * lanes, 2 * lanes)
    table[pad_rows, :] = jnp.zeros((2 * lanes, 128), BF)
    wait_all(copies)

    def stores(t, slot):
        return (pltpu.make_async_copy(x_buf.at[slot], x_out.at[tile_rows(t)], out_sems.at[0, slot]),
                pltpu.make_async_copy(g_buf.at[slot], g_out.at[tile_rows(t)], out_sems.at[1, slot]))

    def tile(t, carry):
        slot = lax.rem(t, DEPTH)
        list_wait(t)

        @pl.when(t >= DEPTH)
        def _():
            wait_all(stores(t - DEPTH, slot))

        gather_tile(lanes, t, table, tok, gate, x_stage, g_stage, x_buf.at[slot], g_buf.at[slot])
        start_all(stores(t, slot))
        return carry

    lax.fori_loop(0, count, tile, 0)
    for back in range(DEPTH, 0, -1):
        @pl.when(count >= back)
        def _():
            wait_all(stores(count - back, lax.rem(count - back, DEPTH)))


def grad_parts(key):
    return 1 if key in EXPERTS[:2] else 3


def part_refs(refs, dim):
    return [refs[0].at[pl.ds(c * dim, dim)] for c in range(3)] if len(refs) == 1 else refs


def row_math(ff, dim, x_rows, g_rows, w_ref, o_dst, dx_dst):
    gate_w = w_ref[0:dim, :]
    up_w = w_ref[dim:2 * dim, :]
    u_val = dot_nn(x_rows, gate_w)
    v_val = dot_nn(x_rows, up_w)
    sig = jax.nn.sigmoid(u_val)
    act = (u_val * sig * v_val).astype(BF)
    d_act = None
    for h in range(dim // ff):
        cols = slice(h * ff, (h + 1) * ff)
        down = w_ref[2 * dim + h * ff:2 * dim + (h + 1) * ff, :]
        o_dst[:, cols] = dot_nn(act, down).astype(BF)
        part = dot_nt(g_rows[:, cols], down)
        d_act = part if d_act is None else d_act + part
    d_u = (d_act * v_val * sig * (1.0 + u_val * (1.0 - sig))).astype(BF)
    d_v = (d_act * u_val * sig).astype(BF)
    dx_dst[...] = (dot_nt(d_u, gate_w) + dot_nt(d_v, up_w)).astype(BF)
    return act, d_u, d_v


def add_grads(ff, dim, p_ref, x_rows, g_rows, act, d_u, d_v):
    p_ref[0:dim, :] += dot_tn(x_rows, d_u)
    p_ref[dim:2 * dim, :] += dot_tn(x_rows, d_v)
    for h in range(dim // ff):
        p_ref[2 * dim + h * ff:2 * dim + (h + 1) * ff, :] += dot_tn(act, g_rows[:, h * ff:(h + 1) * ff])


def deferring_kernel(ff, dim, j0, n, first_tile, n_tiles, x_hbm, g_hbm, *rest):
    w_refs = rest[:n]
    o_hbm, dx_hbm, f_hbm, w_buf, x_buf, g_buf, o_buf, dx_buf, f_buf, w_sem, in_sem, out_sem = rest[n + 2:]
    base = first_tile[j0]
    count = first_tile[j0 + n - 1] + n_tiles[j0 + n - 1] - base

    def loads(t, slot):
        rows = tile_rows(base + t)
        return [pltpu.make_async_copy(ref.at[rows], buf.at[slot], in_sem.at[i, slot]) for i, (ref, buf) in enumerate(((x_hbm, x_buf), (g_hbm, g_buf)))]

    def stores(t, slot):
        rows = tile_rows(base + t)
        return [pltpu.make_async_copy(buf.at[slot], ref.at[rows], out_sem.at[i, slot]) for i, (ref, buf) in enumerate(((o_hbm, o_buf), (dx_hbm, dx_buf), (f_hbm, f_buf)))]

    def w_copy(i):
        return pltpu.make_async_copy(w_refs[i], w_buf.at[i % 2], w_sem.at[i % 2])

    start_all(loads(0, 0))
    w_copy(0).start()

    def tile(t, carry):
        slot = lax.rem(t, 2)
        place = base + t
        which = jnp.int32(0)
        for i in range(1, n):
            which = which + (place >= first_tile[j0 + i]).astype(I32)

        @pl.when(t + 1 < count)
        def _():
            start_all(loads(t + 1, 1 - slot))

        for i in range(n):
            @pl.when(place == first_tile[j0 + i])
            def _():
                w_copy(i).wait()
                if i < n - 1:
                    w_copy(i + 1).start()

        @pl.when(t >= 2)
        def _():
            wait_all(stores(t - 2, slot))

        wait_all(loads(t, slot))
        factors = row_math(ff, dim, x_buf[slot], g_buf[slot], w_buf.at[lax.rem(which, 2)], o_buf.at[slot], dx_buf.at[slot])
        for c, value in enumerate(factors):
            f_buf[slot, :, c * ff:(c + 1) * ff] = value
        start_all(stores(t, slot))
        return carry

    lax.fori_loop(0, count, tile, 0)
    for back in (2, 1):
        @pl.when(count >= back)
        def _():
            wait_all(stores(count - back, lax.rem(count - back, 2)))


def late_grad_kernel(ff, dim, j0, n, first_tile, n_tiles, x_hbm, g_hbm, f_hbm, *rest):
    init_refs = [rest[3 * i:3 * i + 3] for i in range(n)]
    p_refs = [rest[3 * (n + i):3 * (n + i) + 3] for i in range(n)]
    p_buf, x_buf, g_buf, f_buf, i_sem, p_sem, in_sem = rest[6 * n:]
    base = first_tile[j0]
    count = first_tile[j0 + n - 1] + n_tiles[j0 + n - 1] - base

    def loads(t, slot):
        rows = tile_rows(base + t)
        return [pltpu.make_async_copy(ref.at[rows], buf.at[slot], in_sem.at[i, slot]) for i, (ref, buf) in enumerate(((x_hbm, x_buf), (g_hbm, g_buf), (f_hbm, f_buf)))]

    def moves(refs, i, sem, out):
        pairs = [(refs[i][c], p_buf.at[i % 3, pl.ds(c * dim, dim)], sem.at[i % 3, c]) for c in range(3)]
        return [pltpu.make_async_copy(vmem, hbm, s) if out else pltpu.make_async_copy(hbm, vmem, s) for hbm, vmem, s in pairs]

    start_all(loads(0, 0))
    start_all(moves(init_refs, 0, i_sem, False))

    def tile(t, carry):
        slot = lax.rem(t, 2)
        place = base + t
        which = jnp.int32(0)
        for i in range(1, n):
            which = which + (place >= first_tile[j0 + i]).astype(I32)

        @pl.when(t + 1 < count)
        def _():
            start_all(loads(t + 1, 1 - slot))

        for i in range(n):
            @pl.when(place == first_tile[j0 + i])
            def _():
                if i >= 2:
                    wait_all(moves(p_refs, i - 2, p_sem, True))
                if i < n - 1:
                    start_all(moves(init_refs, i + 1, i_sem, False))
                wait_all(moves(init_refs, i, i_sem, False))

        wait_all(loads(t, slot))
        factors = [f_buf[slot, :, c * ff:(c + 1) * ff] for c in range(3)]
        add_grads(ff, dim, p_buf.at[lax.rem(which, 3)], x_buf[slot], g_buf[slot], *factors)

        for i in range(n):
            @pl.when(place == first_tile[j0 + i] + n_tiles[j0 + i] - 1)
            def _():
                start_all(moves(p_refs, i, p_sem, True))
        return carry

    lax.fori_loop(0, count, tile, 0)
    for i in range(max(0, n - 2), n):
        wait_all(moves(p_refs, i, p_sem, True))


def expert_kernel(ff, dim, j0, n, inits, n_carried, first_tile, n_tiles, *rest):
    ins, rest = rest[:2], rest[2:]
    w_refs = rest[:n]
    rest = list(rest[n:])

    def take(key):
        return part_refs([rest.pop(0) for _ in range(grad_parts(key))], dim)

    keys = EXPERTS[j0:j0 + n]
    init_refs = [take(key) if has else None for key, has in zip(keys, inits)]
    rest = rest[n_carried:]
    o_hbm, dx_hbm, *rest = rest
    p_refs = [take(key) for key in keys]
    w_buf, p_buf, x_buf, g_buf, o_buf, dx_buf, w_sem, i_sem, p_sem, in_sem, out_sem = rest
    base = first_tile[j0]
    count = first_tile[j0 + n - 1] + n_tiles[j0 + n - 1] - base

    def loads(t, slot):
        rows = tile_rows(base + t)
        return [pltpu.make_async_copy(ref.at[rows], buf.at[slot], in_sem.at[i, slot]) for i, (ref, buf) in enumerate(zip(ins, (x_buf, g_buf)))]

    def stores(t, slot):
        rows = tile_rows(base + t)
        return (pltpu.make_async_copy(o_buf.at[slot], o_hbm.at[rows], out_sem.at[0, slot]),
                pltpu.make_async_copy(dx_buf.at[slot], dx_hbm.at[rows], out_sem.at[1, slot]))

    def w_copy(i):
        return pltpu.make_async_copy(w_refs[i], w_buf.at[i % 2], w_sem.at[i % 2])

    def init_copy(i):
        return [pltpu.make_async_copy(init_refs[i][c], p_buf.at[i % 3, pl.ds(c * dim, dim)], i_sem.at[i % 3, c]) for c in range(3)]

    def flush(i):
        return [pltpu.make_async_copy(p_buf.at[i % 3, pl.ds(c * dim, dim)], p_refs[i][c], p_sem.at[i % 3, c]) for c in range(3)]

    start_all(loads(0, 0))
    w_copy(0).start()

    def tile(t, carry):
        slot = lax.rem(t, 2)
        place = base + t
        which = jnp.int32(0)
        for i in range(1, n):
            which = which + (place >= first_tile[j0 + i]).astype(I32)

        @pl.when(t + 1 < count)
        def _():
            start_all(loads(t + 1, 1 - slot))

        for i in range(n):
            @pl.when(place == first_tile[j0 + i])
            def _():
                w_copy(i).wait()
                if i == 0 and inits[0]:
                    start_all(init_copy(0))
                if i < n - 1:
                    w_copy(i + 1).start()
                if i >= 2:
                    wait_all(flush(i - 2))
                if i < n - 1 and inits[i + 1]:
                    start_all(init_copy(i + 1))
                if not inits[i]:
                    def clear(r, inner):
                        p_buf[i % 3, pl.ds(pl.multiple_of(r * 64, 64), 64), :] = jnp.zeros((64, ff), F32)
                        return inner

                    lax.fori_loop(0, 3 * dim // 64, clear, 0)

        @pl.when(t >= 2)
        def _():
            wait_all(stores(t - 2, slot))

        wait_all(loads(t, slot))
        factors = row_math(ff, dim, x_buf[slot], g_buf[slot], w_buf.at[lax.rem(which, 2)], o_buf.at[slot], dx_buf.at[slot])
        start_all(stores(t, slot))
        for i in range(n):
            if inits[i]:
                @pl.when(place == first_tile[j0 + i])
                def _():
                    wait_all(init_copy(i))
        add_grads(ff, dim, p_buf.at[lax.rem(which, 3)], x_buf[slot], g_buf[slot], *factors)

        for i in range(n):
            @pl.when(place == first_tile[j0 + i] + n_tiles[j0 + i] - 1)
            def _():
                start_all(flush(i))
        return carry

    lax.fori_loop(0, count, tile, 0)
    for back in (2, 1):
        @pl.when(count >= back)
        def _():
            wait_all(stores(count - back, lax.rem(count - back, 2)))
    for i in range(max(0, n - 2), n):
        wait_all(flush(i))


def combine_kernel(lanes, n_src, use_gate, total, tok_hbm, gate_hbm, rows_hbm, mate_out, own_out, acc, stage, buf, tok, gate, sems, in_sem, list_sems):
    count = total[0]
    list_wait = list_stream(0, count, tok_hbm, gate_hbm, tok, gate, list_sems)

    def load(t, slot):
        return pltpu.make_async_copy(rows_hbm.at[tile_rows(t)], buf.at[slot], in_sem.at[slot])

    for ahead in range(DEPTH - 1):
        @pl.when(ahead < count)
        def _():
            load(ahead, ahead).start()

    def clear(i, carry):
        acc[pl.ds(pl.multiple_of(i * 256, 256), 256), :] = jnp.zeros((256, 128), F32)
        return carry

    lax.fori_loop(0, acc.shape[0] // 256, clear, 0)

    def tile(t, carry):
        slot = lax.rem(t, DEPTH)

        @pl.when(t + DEPTH - 1 < count)
        def _():
            load(t + DEPTH - 1, lax.rem(t + DEPTH - 1, DEPTH)).start()

        list_wait(t)
        load(t, slot).wait()
        for c in range(lanes):
            stage[pl.ds(c, TILE, stride=lanes), :] = buf[slot, :, c * 128:(c + 1) * 128].astype(F32)

        def body(block, inner):
            row0 = block * GROUP
            dests, sums = [], []
            for q in range(GROUP):
                pos = t * TILE + row0 + q
                t_row = pl.ds(pl.multiple_of(tok[pos], lanes), lanes)
                value = stage[pl.ds(pl.multiple_of((row0 + q) * lanes, lanes), lanes), :]
                if use_gate:
                    value = value * gate[pos]
                dests.append(t_row)
                sums.append(acc[t_row, :] + value)
            for t_row, total_row in zip(dests, sums):
                acc[t_row, :] = total_row
            return inner

        lax.fori_loop(0, TILE // GROUP, body, 0)
        return carry

    lax.fori_loop(0, count, tile, 0)
    copies = [pltpu.make_async_copy(acc.at[pl.ds(i * n_src * lanes, n_src * lanes)], ref, sems.at[i]) for i, ref in enumerate((mate_out, own_out))]
    start_all(copies)
    wait_all(copies)


def add_kernel(a_ref, b_ref, out_ref):
    out_ref[...] = a_ref[...] + b_ref[...]


def finish_kernel(lanes, near_ref, x_ref, out_ref, stage):
    rows = near_ref.shape[0] // lanes
    stage[...] = near_ref[...] + x_ref[...]
    for c in range(lanes):
        out_ref[:, c * 128:(c + 1) * 128] = stage[pl.ds(c, rows, stride=lanes), :].astype(BF)


def total_kernel(near_a, far_a, near_b, far_b, out_ref):
    for e, (near, far) in enumerate(((near_a, far_a), (near_b, far_b))):
        value = near[...] + far[...]
        out_ref[e] = jnp.concatenate([value[h] for h in range(value.shape[0])], axis=1)


def solution(mesh):
    n_dev = mesh.shape['ep']

    def permute(value, mask):
        return lax.ppermute(value, 'ep', [(i, i ^ mask) for i in range(n_dev)])

    def call_kernel(body, args, scalars, out_shape, scratch, aliases=None):
        spec = pltpu.PrefetchScalarGridSpec(num_scalar_prefetch=len(scalars), grid=(), in_specs=[HBM] * len(args), out_specs=[HBM] * len(out_shape), scratch_shapes=scratch)
        return pl.pallas_call(body, grid_spec=spec, out_shape=out_shape, input_output_aliases=aliases or {},
                              compiler_params=pltpu.CompilerParams(vmem_limit_bytes=GRANT))(*scalars, *args)

    def layer(x_tok, route_idx, gates, dy_tok, w_gate, w_up, w_down):
        tok_loc, top_k = route_idx.shape
        dim, ff = w_gate.shape[1], w_gate.shape[2]
        experts = w_gate.shape[0] * n_dev
        lanes = dim // 128
        n_exp = len(EXPERTS)
        slot_cap = max(2 * tok_loc * top_k // (experts - 2), tok_loc // 2)
        list_len = n_exp * -(-2 * slot_cap // TILE) * TILE
        n_half = 2 * tok_loc
        me = lax.axis_index('ep')

        w_shape = jax.ShapeDtypeStruct((3 * dim, ff), BF)
        xd_shape = jax.ShapeDtypeStruct((tok_loc // 2, 2 * lanes, 128), BF)
        own_a, own_b = call_kernel(
            functools.partial(pack_kernel, ff), (w_gate, w_up, w_down), (), [w_shape, w_shape], [pltpu.VMEM((2, 3 * dim, ff), BF), DMA((2, 4)), DMA((2, 4))])
        xd_own = call_kernel(
            prep_kernel, (x_tok, dy_tok), (), [xd_shape, xd_shape],
            [pltpu.VMEM((2, tok_loc, dim), BF), pltpu.VMEM((tok_loc, 2 * lanes, 128), BF), pltpu.VMEM((2, TILE * lanes, 128), F32), DMA((2, tok_loc // TILE)), DMA((tok_loc // TILE,))])
        routing = jnp.concatenate([route_idx.T.astype(F32), gates.T.astype(F32)], axis=0)
        rt_xp = permute(routing, 2)
        rt_mate = permute(routing, 1)
        rt_xpm = permute(rt_xp, 1)
        xd_own = [part.reshape(-1, 128) for part in xd_own]
        wts = {(0, 0): own_a, (0, 1): own_b}
        for key, via, mask in (((4, 0), (0, 0), 4), ((8, 1), (0, 1), 8), ((4, 1), (0, 1), 4), ((8, 0), (0, 0), 8), ((12, 0), (8, 0), 4), ((12, 1), (4, 1), 8)):
            wts[key] = permute(wts[via], mask)
        xd_xp = [permute(part, 2) for part in xd_own]
        xd_mate = [permute(part, 1) for part in xd_own]
        xd_xpm = [permute(part, 1) for part in xd_xp]

        rt_all = jnp.stack([jnp.stack([rt_mate, routing]), jnp.stack([rt_xpm, rt_xp])])
        route = rt_all[:, :, :top_k].astype(I32)
        gate_in = rt_all[:, :, top_k:]
        place = (route // 2) ^ me
        slot = jnp.full_like(route, n_exp)
        for j, (mask, which) in enumerate(EXPERTS):
            slot = jnp.where((place == mask) & (route % 2 == which), j, slot)
        token = lax.broadcasted_iota(I32, route.shape, 1) * tok_loc + lax.broadcasted_iota(I32, route.shape, 3)
        first_key = jnp.arange(2, dtype=I32) * (16 * KEY_STEP)
        key = (slot * KEY_STEP + token + first_key[:, None, None, None]).reshape(2, -1)
        counts = jnp.sum((slot.reshape(1, 2, -1) == jnp.arange(n_exp).reshape(n_exp, 1, 1)).astype(I32), axis=2).T
        n_tiles = jnp.maximum(1, (counts + TILE - 1) // TILE)
        need = n_tiles * TILE - counts
        pad_key = jnp.where(jnp.arange(TILE) < need[:, :, None], jnp.arange(n_exp)[:, None] * KEY_STEP + n_half, n_exp * KEY_STEP) + first_key[:, None, None]
        keys = jnp.concatenate([key, pad_key.reshape(2, -1)], axis=1)
        vals = jnp.concatenate([gate_in.reshape(2, -1), jnp.zeros((2, n_exp * TILE), F32)], axis=1)
        keys, vals = lax.sort((keys.reshape(-1), vals.reshape(-1)), num_keys=1)
        per_half = n_half * top_k + n_exp * TILE
        tile_ends = jnp.cumsum(n_tiles, axis=1)
        totals = [tile_ends[h, n_exp - 1:] for h in range(2)]
        toks = [keys[h * per_half:][:list_len] & (KEY_STEP - 1) for h in range(2)]
        lists = [(toks[h] * (2 * lanes), vals[h * per_half:][:list_len]) for h in range(2)]
        places = [tok * lanes for tok in toks]
        tiles = [(tile_ends[h] - n_tiles[h], n_tiles[h]) for h in range(2)]

        row_shape = jax.ShapeDtypeStruct((list_len, dim), BF)
        tile_buf = pltpu.VMEM((2, TILE, dim), BF)
        factor_shape = jax.ShapeDtypeStruct((list_len, 3 * ff), BF)
        factor_buf = pltpu.VMEM((2, TILE, 3 * ff), BF)
        deep_buf = pltpu.VMEM((DEPTH, TILE, dim), BF)
        half_buf = pltpu.VMEM((2, TILE * lanes // 2, 128), F32)
        list_bufs = [pltpu.SMEM((list_len,), I32), pltpu.SMEM((list_len,), F32)]
        list_sems = DMA((2, list_len // LIST_PART))
        table = pltpu.VMEM(((n_half + 8) * 2 * lanes, 128), BF)
        ins = [call_kernel(
            functools.partial(gather_kernel, lanes), (*lists[h], *pieces), (totals[h],), [row_shape, row_shape],
            [table, half_buf, half_buf, deep_buf, deep_buf, *list_bufs, DMA((4,)), DMA((2, DEPTH)), list_sems])
            for h, pieces in enumerate(((*xd_mate, *xd_own), (*xd_xpm, *xd_xp)))]

        grads, outs = {}, [(), ()]
        for i, (half, lo, hi) in enumerate(CALLS):
            n, keys_now = hi - lo, EXPERTS[lo:hi]
            given = [part for k in keys_now if k in grads for part in grads[k]]
            args = [*ins[half], *[wts[k] for k in keys_now], *given, *outs[half]]
            first_alias = 2 + len(args) - 2
            grad_shapes = [jax.ShapeDtypeStruct((3 * dim // grad_parts(k), ff), F32) for k in keys_now for _ in range(grad_parts(k))]
            scratch = [pltpu.VMEM((2, 3 * dim, ff), BF), pltpu.VMEM((3, 3 * dim, ff), F32), tile_buf, tile_buf, tile_buf, tile_buf,
                       DMA((2,)), DMA((3, 3)), DMA((3, 3)), DMA((2, 2)), DMA((2, 2))]
            aliases = {first_alias: 0, first_alias + 1: 1} if outs[half] else None
            if i == DEFERRED:
                args = [*ins[half], *[wts[k] for k in keys_now], *outs[half]]
                *outs[half], factors = call_kernel(
                    functools.partial(deferring_kernel, ff, dim, lo, n), args, tiles[half], [row_shape, row_shape, factor_shape],
                    [pltpu.VMEM((2, 3 * dim, ff), BF), tile_buf, tile_buf, tile_buf, tile_buf, factor_buf, DMA((2,)), DMA((2, 2)), DMA((3, 2))],
                    {2 + n + 2: 0, 2 + n + 3: 1})
                continue
            body = functools.partial(expert_kernel, ff, dim, lo, n, tuple(k in grads for k in keys_now), len(outs[half]))
            parts = call_kernel(body, args, tiles[half], [row_shape, row_shape] + grad_shapes, scratch, aliases)
            outs[half], parts = parts[:2], parts[2:]
            for k in keys_now:
                grads[k], parts = tuple(parts[:grad_parts(k)]), parts[grad_parts(k):]
        half, lo, hi = CALLS[DEFERRED]
        late = EXPERTS[lo:hi]
        parts = call_kernel(
            functools.partial(late_grad_kernel, ff, dim, lo, hi - lo), [*ins[half], factors, *[part for k in late for part in grads[k]]], tiles[half],
            [jax.ShapeDtypeStruct((dim, ff), F32)] * (3 * (hi - lo)),
            [pltpu.VMEM((3, 3 * dim, ff), F32), tile_buf, tile_buf, factor_buf, DMA((3, 3)), DMA((3, 3)), DMA((3, 2))])
        for m, k in enumerate(late):
            grads[k] = tuple(parts[3 * m:3 * m + 3])

        def combine(half, which, use_gate):
            block = jax.ShapeDtypeStruct((tok_loc * lanes, 128), F32)
            return call_kernel(
                functools.partial(combine_kernel, lanes, tok_loc, use_gate), (places[half], lists[half][1], outs[half][which]), (totals[half],), [block, block],
                [pltpu.VMEM(((n_half + 32) * lanes, 128), F32), pltpu.VMEM((TILE * lanes, 128), F32), deep_buf, *list_bufs, DMA((2,)), DMA((DEPTH,)), list_sems])

        def blocked(body, args, out_shape, in_block, out_block, steps, scratch=()):
            def spec(block):
                axis = 1 if len(block) == 3 else 0
                return pl.BlockSpec(block, lambda i: tuple(i if d == axis else 0 for d in range(len(block))))

            return pl.pallas_call(body, grid=(steps,), in_specs=[spec(in_block)] * len(args), out_specs=spec(out_block), out_shape=out_shape, scratch_shapes=scratch,
                                  compiler_params=pltpu.CompilerParams(vmem_limit_bytes=GRANT))(*args)

        row_block = (TILE * lanes, 128)
        steps = tok_loc // TILE

        def settle_rows(which, use_gate):
            mate1, own1 = combine(1, which, use_gate)
            to_x = blocked(add_kernel, (own1, permute(mate1, 1)), jax.ShapeDtypeStruct((tok_loc * lanes, 128), F32), row_block, row_block, steps)
            from_x = permute(to_x, 2)
            mate0, own0 = combine(0, which, use_gate)
            near_sum = own0 + permute(mate0, 1)
            return blocked(functools.partial(finish_kernel, lanes), (near_sum, from_x), jax.ShapeDtypeStruct((tok_loc, dim), BF), row_block, (TILE, dim), steps,
                           (pltpu.VMEM((TILE * lanes, 128), F32),))

        y_tok = settle_rows(0, True)
        dx_tok = settle_rows(1, False)

        whole_a = permute(grads[(4, 0)][0], 4)
        whole_b = permute(grads[(8, 1)][0], 8)
        sums = []
        for c in range(3):
            def back(key, mask, value=None):
                return permute(grads[key][c] if value is None else value, mask)

            via_a = grads[(8, 0)][c] + back((12, 0), 4)
            via_b = grads[(4, 1)][c] + back((12, 1), 8)
            part = slice(c * dim, (c + 1) * dim)
            near_a = grads[(0, 0)][c] + whole_a[part]
            near_b = grads[(0, 1)][c] + whole_b[part]
            parts = (near_a, back((8, 0), 8, via_a), near_b, back((4, 1), 4, via_b))
            wide = dim // ff if c == 2 else 1
            rows = dim // wide
            sums.append(blocked(total_kernel, [p.reshape(wide, rows, ff) for p in parts], jax.ShapeDtypeStruct((2, rows, wide * ff), F32),
                                (wide, 128, ff), (2, 128, wide * ff), rows // 128))
        return y_tok, dx_tok, *sums

    return jax.shard_map(layer, mesh=mesh, in_specs=(P('ep'),) * 7, out_specs=(P('ep'),) * 5, check_vma=False)
```

time: 1140 us -> 1290 us (1.13)
  waiting for transfers between devices: 574 us -> 693 us
  Pallas kernels: 400 us -> 447 us
  local copies, waits for them, and re-layouts: 18.5 us -> 3.98 us
    ppermute x39 -> x35, waiting for transfers between devices: 574 us -> 693 us  [permute(): return lax.ppermute(value, 'ep', [(i, i ^ mask) for i in range(n_dev)])]
    pallas_call x15 -> x22, Pallas kernels: 400 us -> 447 us  [the longest x15 394 us: call_kernel(): pl.pallas_call(body, grid_spec=spec, out_shape=out_shape, input_output_al...]
    another operation x9 -> x0, other arithmetic: 23.1 us -> none  [layer(): totals.append(jnp.stack([g_a, g_b]))]
    add x2 -> x4, other arithmetic: 8.14 us -> 25.6 us  [the longest x2 12.7 us: settle_rows(): near_sum = own0 + permute(mate0, 1)]
    ppermute x39 -> x35, starting transfers between devices: 40.5 us -> 49.2 us  [permute(): return lax.ppermute(value, 'ep', [(i, i ^ mask) for i in range(n_dev)])]
  transfers between devices with their start and end apart: 39 -> 35, of which waited for: 15 -> 12; matrix products, arithmetic and copies ran while one was open for 9% -> 7% of each run, Pallas kernels for 35% -> 30%
where the time goes in v3:
time: 1290 us; the launch traced here: 1280 us
  waiting for transfers between devices  693 us (54%)
  Pallas kernels  447 us (35%)
  other arithmetic  88.1 us (7%)
  starting transfers between devices  49.2 us (4%)
    ppermute x35, waiting for transfers between devices, permute(): return lax.ppermute(value, 'ep', [(i, i ^ mask) for i in range(n_dev)])  693 us
    pallas_call x15, Pallas kernels, call_kernel(): pl.pallas_call(body, grid_spec=spec, out_shape=out_shape, input_output_al...  394 us
    pallas_call x7, Pallas kernels, blocked(): pl.pallas_call(body, grid=(steps,), in_specs=[spec(in_block)] * len(args)...  53.3 us
    ppermute x35, starting transfers between devices, permute(): return lax.ppermute(value, 'ep', [(i, i ^ mask) for i in range(n_dev)])  49.2 us
    sort x1, other arithmetic, layer(): keys, vals = lax.sort((keys.reshape(-1), vals.reshape(-1)), num_keys=1)  39.8 us
  transfers between devices with their start and end apart: 35, of which 12 were waited for; matrix products, arithmetic and copies ran while one was open for 7% of the time, Pallas kernels for 30%

profile of v3, /device:TPU:0, one launch (start us, length us, event | category | flops | bytes accessed | tf_op | source)
XLA Modules:
  0.0 1282.6 jit_solution(3217232509068101641)
XLA Ops:
  10.9 69.8 %collective-permute-done.1 = f32[16,1536]{1,0:T(8,128)S(1)} collective-permute-done((f32[16,1536]{1,0:T(8,128)S(1)}, f32[16,1536]{1,0:T(8,128)S(1)}, u32[]{:S(2)}, u32[]{:S(2)}) %collective-permute-start.1) | collective-permute-done | bytes 98336 | tf_op jit(solution)/shard_map/ppermute | solution.py:490
  91.8 59.8 %collective-permute-done.9.rest_2_ = bf16[12288,128]{1,0:T(8,128)(2,1)} collective-permute-done((bf16[12288,128]{1,0:T(8,128)(2,1)}, bf16[12288,128]{1,0:T(8,128)(2,1)}, u32[]{:S(2)}, u32[]{:S(2)}) %collective-permute-start.9) | collective-permute-done | bytes 3145760 | tf_op jit(solution)/shard_map/ppermute | solution.py:490
  161.3 65.4 %collective-permute-done.6.rest_3_ = bf16[3072,512]{1,0:T(8,128)(2,1)} collective-permute-done((bf16[3072,512]{1,0:T(8,128)(2,1)}, bf16[3072,512]{1,0:T(8,128)(2,1)}, u32[]{:S(2)}, u32[]{:S(2)}) %collective-permute-start.6) | collective-permute-done | bytes 3145760 | tf_op jit(solution)/shard_map/ppermute | solution.py:490
  230.8 39.8 %sort.23 = (s32[53248]{0:T(1024)S(1)}, f32[53248]{0:T(1024)S(1)}, s32[53248]{0:T(1024)}) sort(s32[53248]{0:T(1024)S(1)} %bitcast.91, f32[53248]{0:T(1024)} %bitcast.92, s32[53248]{0:T(1024)S(1)} %iota.41), dimensions={0}, to_apply=%region_2.3 | sort | flops 851968 | bytes 1277952 | tf_op jit(solution)/shard_map/sort | solution.py:543
  273.8 27.0 %shard_map.111 = (bf16[14336,1024]{1,0:T(8,128)(2,1)}, bf16[14336,1024]{1,0:T(8,128)(2,1)}) custom-call(s32[1]{0:T(128)} %bitcast.9.total, s32[14336]{0:T(1024)} %get-tuple-element.160.tok_hbm, f32[14336]{0:T(1024)} %get-tuple-element.164.gate_hbm, bf16[12288,128]{1,0:T(8,128)(2,1)} %collective-permute-done.3.rest_0_, ...), custom_call_target="tpu_custom_call" | custom-call | tf_op jit(solution)/shard_map/pallas_call | solution.py:494
  300.8 48.7 %shard_map.114 = (bf16[14336,1024]{1,0:T(8,128)(2,1)}, bf16[14336,1024]{1,0:T(8,128)(2,1)}, f32[3072,512]{1,0:T(8,128)}, f32[3072,512]{1,0:T(8,128)}, f32[1024,5...) custom-call(s32[8]{0:T(128)} %get-tuple-element.168.first_tile, ...), custom_call_target="tpu_custom_call" | custom-call | tf_op jit(solution)/shard_map/pallas_call | solution.py:494
  349.6 28.0 %shard_map.113 = (bf16[14336,1024]{1,0:T(8,128)(2,1)}, bf16[14336,1024]{1,0:T(8,128)(2,1)}) custom-call(s32[1]{0:T(128)} %bitcast.16.total, s32[14336]{0:T(1024)} %get-tuple-element.161.tok_hbm, f32[14336]{0:T(1024)} %get-tuple-element.163.gate_hbm, bf16[12288,128]{1,0:T(8,128)(2,1)} %collective-permute-done.10.rest_0_, ...), custom_call_target="tpu_custom_call" | custom-call | tf_op jit(solution)/shard_map/pallas_call | solution.py:494
  377.6 25.0 %shard_map.115 = (bf16[14336,1024]{1,0:T(8,128)(2,1)}, bf16[14336,1024]{1,0:T(8,128)(2,1)}, f32[3072,512]{1,0:T(8,128)}, f32[3072,512]{1,0:T(8,128)}) custom-call(s32[8]{0:T(128)} %get-tuple-element.167.first_tile, s32[8]{0:T(128)} %get-tuple-element.171.n_tiles, bf16[14336,1024]{1,0:T(8,128)(2,1)} %get-tuple-element.86.rest_0_.x_hbm, ...), custom_call_target="tpu_custom_call" | custom-call | tf_op jit(solution)/shard_map/pallas_call | solution.py:494
  402.6 35.9 %shard_map.116 = (bf16[14336,1024]{1,0:T(8,128)(2,1)}, bf16[14336,1024]{1,0:T(8,128)(2,1)}, bf16[14336,1536]{1,0:T(8,128)(2,1)}) custom-call(s32[8]{0:T(128)} %get-tuple-element.167.first_tile, s32[8]{0:T(128)} %get-tuple-element.171.n_tiles, bf16[14336,1024]{1,0:T(8,128)(2,1)} %get-tuple-element.86.rest_0_.x_hbm, ...), custom_call_target="tpu_custom_call", output_to_operand_aliasing={{0}: (8, {}), {1}: (9, {})} | custom-call | tf_op jit(solution)/shard_map/pallas_call | solution.py:494
  438.5 23.8 %shard_map.117 = (bf16[14336,1024]{1,0:T(8,128)(2,1)}, bf16[14336,1024]{1,0:T(8,128)(2,1)}, f32[1024,512]{1,0:T(8,128)}, f32[1024,512]{1,0:T(8,128)}, f32[1024,5...) custom-call(s32[8]{0:T(128)} %get-tuple-element.167.first_tile, ...), custom_call_target="tpu_custom_call", output_to_operand_aliasing={{0}: (6, {}), {1}: (7, {})} | custom-call | tf_op jit(solution)/shard_map/pallas_call | solution.py:494
  462.3 25.4 %shard_map.118 = (bf16[14336,1024]{1,0:T(8,128)(2,1)}, bf16[14336,1024]{1,0:T(8,128)(2,1)}, f32[1024,512]{1,0:T(8,128)}, f32[1024,512]{1,0:T(8,128)}, f32[1024,5...) custom-call(s32[8]{0:T(128)} %get-tuple-element.168.first_tile, ...), custom_call_target="tpu_custom_call", output_to_operand_aliasing={{0}: (12, {}), {1}: (13, {})} | custom-call | tf_op jit(solution)/shard_map/pallas_call | solution.py:494
  500.7 29.6 %shard_map.121 = (f32[12288,128]{1,0:T(8,128)}, f32[12288,128]{1,0:T(8,128)}) custom-call(s32[1]{0:T(128)} %bitcast.16.total, s32[14336]{0:T(1024)} %get-tuple-element.159.tok_hbm, f32[14336]{0:T(1024)} %get-tuple-element.163.gate_hbm, bf16[14336,1024]{1,0:T(8,128)(2,1)} %get-tuple-element.107.rows_hbm), custom_call_target="tpu_custom_call" | custom-call | tf_op jit(solution)/shard_map/pallas_call | solution.py:494
  536.5 23.9 %shard_map.119 = (bf16[14336,1024]{1,0:T(8,128)(2,1)}, bf16[14336,1024]{1,0:T(8,128)(2,1)}, f32[1024,512]{1,0:T(8,128)}, f32[1024,512]{1,0:T(8,128)}, f32[1024,5...) custom-call(s32[8]{0:T(128)} %get-tuple-element.168.first_tile, ...), custom_call_target="tpu_custom_call", output_to_operand_aliasing={{0}: (6, {}), {1}: (7, {})} | custom-call | tf_op jit(solution)/shard_map/pallas_call | solution.py:494
  560.4 12.9 %collective-permute-start.33 = (f32[1024,512]{1,0:T(8,128)}, f32[1024,512]{1,0:T(8,128)}, u32[]{:S(2)}, u32[]{:S(2)}) collective-permute-start(f32[1024,512]{1,0:T(8,128)} %get-tuple-element.148), channel_id=1, source_target_pairs={{0,8},{1,9},{2,10},{3,11},{4,12},{5,13},{6,14},{7,15},{8,0},{9,1},... | collective-permute-start | bytes 6291464 | tf_op jit(solution)/shard_map/ppermute | solution.py:490
  573.3 34.3 %shard_map.128 = (f32[1024,512]{1,0:T(8,128)}, f32[1024,512]{1,0:T(8,128)}, f32[1024,512]{1,0:T(8,128)}, f32[1024,512]{1,0:T(8,128)}, f32[1024,512]{1,0:T(8,128)...) custom-call(s32[8]{0:T(128)} %get-tuple-element.167.first_tile, ...), custom_call_target="tpu_custom_call" | custom-call | tf_op jit(solution)/shard_map/pallas_call | solution.py:494
  611.6 26.1 %shard_map.125 = (f32[12288,128]{1,0:T(8,128)}, f32[12288,128]{1,0:T(8,128)}) custom-call(s32[1]{0:T(128)} %bitcast.16.total, s32[14336]{0:T(1024)} %get-tuple-element.159.tok_hbm, f32[14336]{0:T(1024)} %get-tuple-element.163.gate_hbm, bf16[14336,1024]{1,0:T(8,128)(2,1)} %get-tuple-element.113.rows_hbm), custom_call_target="tpu_custom_call" | custom-call | tf_op jit(solution)/shard_map/pallas_call | solution.py:494
  645.0 34.4 %collective-permute-done.23 = f32[1024,512]{1,0:T(8,128)} collective-permute-done((f32[1024,512]{1,0:T(8,128)}, f32[1024,512]{1,0:T(8,128)}, u32[]{:S(2)}, u32[]{:S(2)}) %collective-permute-start.23) | collective-permute-done | bytes 2097184 | tf_op jit(solution)/shard_map/ppermute | solution.py:490
  681.4 139.5 %collective-permute-done.26 = f32[1024,512]{1,0:T(8,128)S(1)} collective-permute-done((f32[1024,512]{1,0:T(8,128)S(1)}, f32[1024,512]{1,0:T(8,128)S(1)}, u32[]{:S(2)}, u32[]{:S(2)}) %collective-permute-start.26) | collective-permute-done | bytes 2097184 | tf_op jit(solution)/shard_map/ppermute | solution.py:490
  830.6 28.7 %shard_map.120 = (f32[12288,128]{1,0:T(8,128)}, f32[12288,128]{1,0:T(8,128)}) custom-call(s32[1]{0:T(128)} %bitcast.9.total, s32[14336]{0:T(1024)} %get-tuple-element.162.tok_hbm, f32[14336]{0:T(1024)} %get-tuple-element.164.gate_hbm, bf16[14336,1024]{1,0:T(8,128)(2,1)} %get-tuple-element.104.rows_hbm), custom_call_target="tpu_custom_call" | custom-call | tf_op jit(solution)/shard_map/pallas_call | solution.py:494
  859.2 25.5 %shard_map.124 = (f32[12288,128]{1,0:T(8,128)}, f32[12288,128]{1,0:T(8,128)}) custom-call(s32[1]{0:T(128)} %bitcast.9.total, s32[14336]{0:T(1024)} %get-tuple-element.162.tok_hbm, f32[14336]{0:T(1024)} %get-tuple-element.164.gate_hbm, bf16[14336,1024]{1,0:T(8,128)(2,1)} %get-tuple-element.110.rows_hbm), custom_call_target="tpu_custom_call" | custom-call | tf_op jit(solution)/shard_map/pallas_call | solution.py:494
  902.0 101.2 %collective-permute-done.32 = f32[1024,512]{1,0:T(8,128)} collective-permute-done((f32[1024,512]{1,0:T(8,128)}, f32[1024,512]{1,0:T(8,128)}, u32[]{:S(2)}, u32[]{:S(2)}) %collective-permute-start.32) | collective-permute-done | bytes 2097184 | tf_op jit(solution)/shard_map/ppermute | solution.py:490
  1037.9 17.5 %collective-permute-done.34 = f32[1024,512]{1,0:T(8,128)} collective-permute-done((f32[1024,512]{1,0:T(8,128)}, f32[1024,512]{1,0:T(8,128)}, u32[]{:S(2)}, u32[]{:S(2)}) %collective-permute-start.34) | collective-permute-done | bytes 2097184 | tf_op jit(solution)/shard_map/ppermute | solution.py:490
  1074.5 67.4 %collective-permute-done.17.x_ref = f32[12288,128]{1,0:T(8,128)} collective-permute-done((f32[12288,128]{1,0:T(8,128)}, f32[12288,128]{1,0:T(8,128)}, u32[]{:S(2)}, u32[]{:S(2)}) %collective-permute-start.17) | collective-permute-done | bytes 6291488 | tf_op jit(solution)/shard_map/ppermute | solution.py:490
  1149.7 124.7 %collective-permute-done.20.x_ref = f32[12288,128]{1,0:T(8,128)} collective-permute-done((f32[12288,128]{1,0:T(8,128)}, f32[12288,128]{1,0:T(8,128)}, u32[]{:S(2)}, u32[]{:S(2)}) %collective-permute-start.20) | collective-permute-done | bytes 6291488 | tf_op jit(solution)/shard_map/ppermute | solution.py:490
  (144 shorter events, 167.3 us)
Async XLA Ops:
  7.1 82.5 %collective-permute-start.11 = (bf16[12288,128]{1,0:T(8,128)(2,1)}, bf16[12288,128]{1,0:T(8,128)(2,1)}, u32[]{:S(2)}, u32[]{:S(2)}) collective-permute-start(bf16[12288,128]{1,0:T(8,128)(2,1)} %bitcast.86), channel_id=1, source_target_pairs={{0,2},{1,3},{2,0},{3,1},{4,6},{5,7},{6,4},{7,5},{8,10},{9,11},{10,... | collective-permute-start | bytes 9437192 | tf_op jit(solution)/shard_map/ppermute | solution.py:490
  10.3 80.8 %collective-permute-start.4 = (bf16[12288,128]{1,0:T(8,128)(2,1)}, bf16[12288,128]{1,0:T(8,128)(2,1)}, u32[]{:S(2)}, u32[]{:S(2)}) collective-permute-start(bf16[12288,128]{1,0:T(8,128)(2,1)} %bitcast.87), channel_id=1, source_target_pairs={{0,1},{1,0},{2,3},{3,2},{4,5},{5,4},{6,7},{7,6},{8,9},{9,8},{10,11... | collective-permute-start | bytes 9437192 | tf_op jit(solution)/shard_map/ppermute | solution.py:490
  10.5 77.3 %collective-permute-start = (f32[16,1536]{1,0:T(8,128)S(1)}, f32[16,1536]{1,0:T(8,128)S(1)}, u32[]{:S(2)}, u32[]{:S(2)}) collective-permute-start(f32[16,1536]{1,0:T(8,128)S(1)} %get-tuple-element.166), channel_id=1, source_target_pairs={{0,1},{1,0},{2,3},{3,2},{4,5},{5,4},{6,7},{7,6},{8,9},{9,8},{10,11... | collective-permute-start | bytes 294920 | tf_op jit(solution)/shard_map/ppermute | solution.py:490
  91.1 135.6 %collective-permute-start.6 = (bf16[3072,512]{1,0:T(8,128)(2,1)}, bf16[3072,512]{1,0:T(8,128)(2,1)}, u32[]{:S(2)}, u32[]{:S(2)}) collective-permute-start(bf16[3072,512]{1,0:T(8,128)(2,1)} %get-tuple-element.85.rest_5_.rest_1_), channel_id=1, source_target_pairs={{0,4},{1,5},{2,6},{3,7},{4,0},{5,1},{6,2},{7,3},{8,12},{9,13},{10,... | collective-permute-start | bytes 9437192 | tf_op jit(solution)/shard_map/ppermute | solution.py:490
  151.5 149.3 %collective-permute-start.14 = (bf16[3072,512]{1,0:T(8,128)(2,1)}, bf16[3072,512]{1,0:T(8,128)(2,1)}, u32[]{:S(2)}, u32[]{:S(2)}) collective-permute-start(bf16[3072,512]{1,0:T(8,128)(2,1)} %get-tuple-element.85.rest_5_.rest_1_), channel_id=1, source_target_pairs={{0,8},{1,9},{2,10},{3,11},{4,12},{5,13},{6,14},{7,15},{8,0},{9,1},... | collective-permute-start | bytes 9437192 | tf_op jit(solution)/shard_map/ppermute | solution.py:490
  153.4 196.2 %collective-permute-start.12 = (bf16[12288,128]{1,0:T(8,128)(2,1)}, bf16[12288,128]{1,0:T(8,128)(2,1)}, u32[]{:S(2)}, u32[]{:S(2)}) collective-permute-start(bf16[12288,128]{1,0:T(8,128)(2,1)} %collective-permute-done.11.rest_3_), channel_id=1, source_target_pairs={{0,1},{1,0},{2,3},{3,2},{4,5},{5,4},{6,7},{7,6},{8,9},{9,8},{10,11... | collective-permute-start | bytes 9437192 | tf_op jit(solution)/shard_map/ppermute | solution.py:490
  159.2 190.4 %collective-permute-start.10 = (bf16[12288,128]{1,0:T(8,128)(2,1)}, bf16[12288,128]{1,0:T(8,128)(2,1)}, u32[]{:S(2)}, u32[]{:S(2)}) collective-permute-start(bf16[12288,128]{1,0:T(8,128)(2,1)} %collective-permute-done.9.rest_2_), channel_id=1, source_target_pairs={{0,1},{1,0},{2,3},{3,2},{4,5},{5,4},{6,7},{7,6},{8,9},{9,8},{10,11... | collective-permute-start | bytes 9437192 | tf_op jit(solution)/shard_map/ppermute | solution.py:490
  160.8 277.6 %collective-permute-start.7 = (bf16[3072,512]{1,0:T(8,128)(2,1)}, bf16[3072,512]{1,0:T(8,128)(2,1)}, u32[]{:S(2)}, u32[]{:S(2)}) collective-permute-start(bf16[3072,512]{1,0:T(8,128)(2,1)} %collective-permute-done.5.rest_2_), channel_id=1, source_target_pairs={{0,4},{1,5},{2,6},{3,7},{4,0},{5,1},{6,2},{7,3},{8,12},{9,13},{10,... | collective-permute-start | bytes 9437192 | tf_op jit(solution)/shard_map/ppermute | solution.py:490
  226.7 211.7 %collective-permute-start.8 = (bf16[3072,512]{1,0:T(8,128)(2,1)}, bf16[3072,512]{1,0:T(8,128)(2,1)}, u32[]{:S(2)}, u32[]{:S(2)}) collective-permute-start(bf16[3072,512]{1,0:T(8,128)(2,1)} %collective-permute-done.6.rest_3_), channel_id=1, source_target_pairs={{0,8},{1,9},{2,10},{3,11},{4,12},{5,13},{6,14},{7,15},{8,0},{9,1},... | collective-permute-start | bytes 9437192 | tf_op jit(solution)/shard_map/ppermute | solution.py:490
  500.5 111.0 %collective-permute-start.27 = (f32[1024,512]{1,0:T(8,128)}, f32[1024,512]{1,0:T(8,128)}, u32[]{:S(2)}, u32[]{:S(2)}) collective-permute-start(f32[1024,512]{1,0:T(8,128)} %get-tuple-element.139), channel_id=1, source_target_pairs={{0,4},{1,5},{2,6},{3,7},{4,0},{5,1},{6,2},{7,3},{8,12},{9,13},{10,... | collective-permute-start | bytes 6291464 | tf_op jit(solution)/shard_map/ppermute | solution.py:490
  500.6 137.1 %collective-permute-start.29 = (f32[1024,512]{1,0:T(8,128)}, f32[1024,512]{1,0:T(8,128)}, u32[]{:S(2)}, u32[]{:S(2)}) collective-permute-start(f32[1024,512]{1,0:T(8,128)} %get-tuple-element.142), channel_id=1, source_target_pairs={{0,8},{1,9},{2,10},{3,11},{4,12},{5,13},{6,14},{7,15},{8,0},{9,1},... | collective-permute-start | bytes 6291464 | tf_op jit(solution)/shard_map/ppermute | solution.py:490
  530.2 298.9 %collective-permute-start.16 = (f32[12288,128]{1,0:T(8,128)}, f32[12288,128]{1,0:T(8,128)}, u32[]{:S(2)}, u32[]{:S(2)}) collective-permute-start(f32[12288,128]{1,0:T(8,128)} %get-tuple-element.109), channel_id=1, source_target_pairs={{0,1},{1,0},{2,3},{3,2},{4,5},{5,4},{6,7},{7,6},{8,9},{9,8},{10,11... | collective-permute-start | bytes 18874376 | tf_op jit(solution)/shard_map/ppermute | solution.py:490
  536.5 101.2 %collective-permute-start.31 = (f32[1024,512]{1,0:T(8,128)}, f32[1024,512]{1,0:T(8,128)}, u32[]{:S(2)}, u32[]{:S(2)}) collective-permute-start(f32[1024,512]{1,0:T(8,128)} %get-tuple-element.145), channel_id=1, source_target_pairs={{0,4},{1,5},{2,6},{3,7},{4,0},{5,1},{6,2},{7,3},{8,12},{9,13},{10,... | collective-permute-start | bytes 6291464 | tf_op jit(solution)/shard_map/ppermute | solution.py:490
  560.4 80.3 %collective-permute-start.33 = (f32[1024,512]{1,0:T(8,128)}, f32[1024,512]{1,0:T(8,128)}, u32[]{:S(2)}, u32[]{:S(2)}) collective-permute-start(f32[1024,512]{1,0:T(8,128)} %get-tuple-element.148), channel_id=1, source_target_pairs={{0,8},{1,9},{2,10},{3,11},{4,12},{5,13},{6,14},{7,15},{8,0},{9,1},... | collective-permute-start | bytes 6291464 | tf_op jit(solution)/shard_map/ppermute | solution.py:490
  637.7 255.4 %collective-permute-start.19 = (f32[12288,128]{1,0:T(8,128)}, f32[12288,128]{1,0:T(8,128)}, u32[]{:S(2)}, u32[]{:S(2)}) collective-permute-start(f32[12288,128]{1,0:T(8,128)} %get-tuple-element.115), channel_id=1, source_target_pairs={{0,1},{1,0},{2,3},{3,2},{4,5},{5,4},{6,7},{7,6},{8,9},{9,8},{10,11... | collective-permute-start | bytes 18874376 | tf_op jit(solution)/shard_map/ppermute | solution.py:490
  637.8 365.3 %collective-permute-start.21 = (f32[3072,512]{1,0:T(8,128)}, f32[3072,512]{1,0:T(8,128)}, u32[]{:S(2)}, u32[]{:S(2)}) collective-permute-start(f32[3072,512]{1,0:T(8,128)} %get-tuple-element.130), channel_id=1, source_target_pairs={{0,4},{1,5},{2,6},{3,7},{4,0},{5,1},{6,2},{7,3},{8,12},{9,13},{10,... | collective-permute-start | bytes 18874376 | tf_op jit(solution)/shard_map/ppermute | solution.py:490
  640.7 180.1 %collective-permute-start.26 = (f32[1024,512]{1,0:T(8,128)S(1)}, f32[1024,512]{1,0:T(8,128)S(1)}, u32[]{:S(2)}, u32[]{:S(2)}) collective-permute-start(f32[1024,512]{1,0:T(8,128)S(1)} %add.112), channel_id=1, source_target_pairs={{0,4},{1,5},{2,6},{3,7},{4,0},{5,1},{6,2},{7,3},{8,12},{9,13},{10,... | collective-permute-start | bytes 6291464 | tf_op jit(solution)/shard_map/ppermute | solution.py:490
  679.4 145.6 %collective-permute-start.28 = (f32[1024,512]{1,0:T(8,128)S(1)}, f32[1024,512]{1,0:T(8,128)S(1)}, u32[]{:S(2)}, u32[]{:S(2)}) collective-permute-start(f32[1024,512]{1,0:T(8,128)S(1)} %add.114), channel_id=1, source_target_pairs={{0,8},{1,9},{2,10},{3,11},{4,12},{5,13},{6,14},{7,15},{8,0},{9,1},... | collective-permute-start | bytes 6291464 | tf_op jit(solution)/shard_map/ppermute | solution.py:490
  820.8 188.5 %collective-permute-start.24 = (f32[3072,512]{1,0:T(8,128)}, f32[3072,512]{1,0:T(8,128)}, u32[]{:S(2)}, u32[]{:S(2)}) collective-permute-start(f32[3072,512]{1,0:T(8,128)} %get-tuple-element.134), channel_id=1, source_target_pairs={{0,8},{1,9},{2,10},{3,11},{4,12},{5,13},{6,14},{7,15},{8,0},{9,1},... | collective-permute-start | bytes 18874376 | tf_op jit(solution)/shard_map/ppermute | solution.py:490
  829.1 174.0 %collective-permute-start.32 = (f32[1024,512]{1,0:T(8,128)}, f32[1024,512]{1,0:T(8,128)}, u32[]{:S(2)}, u32[]{:S(2)}) collective-permute-start(f32[1024,512]{1,0:T(8,128)} %add.118), channel_id=1, source_target_pairs={{0,8},{1,9},{2,10},{3,11},{4,12},{5,13},{6,14},{7,15},{8,0},{9,1},... | collective-permute-start | bytes 6291464 | tf_op jit(solution)/shard_map/ppermute | solution.py:490
  893.1 168.0 %collective-permute-start.15 = (f32[12288,128]{1,0:T(8,128)}, f32[12288,128]{1,0:T(8,128)}, u32[]{:S(2)}, u32[]{:S(2)}) collective-permute-start(f32[12288,128]{1,0:T(8,128)} %get-tuple-element.106), channel_id=1, source_target_pairs={{0,1},{1,0},{2,3},{3,2},{4,5},{5,4},{6,7},{7,6},{8,9},{9,8},{10,11... | collective-permute-start | bytes 18874376 | tf_op jit(solution)/shard_map/ppermute | solution.py:490
  893.1 175.9 %collective-permute-start.18 = (f32[12288,128]{1,0:T(8,128)}, f32[12288,128]{1,0:T(8,128)}, u32[]{:S(2)}, u32[]{:S(2)}) collective-permute-start(f32[12288,128]{1,0:T(8,128)} %get-tuple-element.112), channel_id=1, source_target_pairs={{0,1},{1,0},{2,3},{3,2},{4,5},{5,4},{6,7},{7,6},{8,9},{9,8},{10,11... | collective-permute-start | bytes 18874376 | tf_op jit(solution)/shard_map/ppermute | solution.py:490
  1003.1 138.7 %collective-permute-start.17 = (f32[12288,128]{1,0:T(8,128)}, f32[12288,128]{1,0:T(8,128)}, u32[]{:S(2)}, u32[]{:S(2)}) collective-permute-start(f32[12288,128]{1,0:T(8,128)} %shard_map.122), channel_id=1, source_target_pairs={{0,2},{1,3},{2,0},{3,1},{4,6},{5,7},{6,4},{7,5},{8,10},{9,11},{10,... | collective-permute-start | bytes 18874376 | tf_op jit(solution)/shard_map/ppermute | solution.py:490
  1003.1 271.3 %collective-permute-start.20 = (f32[12288,128]{1,0:T(8,128)}, f32[12288,128]{1,0:T(8,128)}, u32[]{:S(2)}, u32[]{:S(2)}) collective-permute-start(f32[12288,128]{1,0:T(8,128)} %shard_map.126), channel_id=1, source_target_pairs={{0,2},{1,3},{2,0},{3,1},{4,6},{5,7},{6,4},{7,5},{8,10},{9,11},{10,... | collective-permute-start | bytes 18874376 | tf_op jit(solution)/shard_map/ppermute | solution.py:490
  (27 other events, 997.1 us)
